TPU v7x, 32 devices: a whole 2x2x4 slice. The times are simulated.
32 devices in a mesh: rep: 4 (over x, y), dp: 8 (over z, core).
Axes of the slice: x: 2, y: 2, z: 4, core: 2. Of those that a mesh axis runs over, the one named last changes fastest.
Arguments:
- x: bfloat16 [32, 2048, 640], P(('rep', 'dp')), parts along dimension 0
- dy: bfloat16 [32, 2048, 640], P(('rep', 'dp')), parts along dimension 0
- w_gate: bfloat16 [2, 640, 2432], replicated
- w_up: bfloat16 [2, 640, 2432], replicated
- w_down: bfloat16 [2, 2432, 640], replicated
- m_w_gate: float32 [2, 640, 2432], replicated
- m_w_up: float32 [2, 640, 2432], replicated
- m_w_down: float32 [2, 2432, 640], replicated
- v_w_gate: float32 [2, 640, 2432], replicated
- v_w_up: float32 [2, 640, 2432], replicated
- v_w_down: float32 [2, 2432, 640], replicated
Outputs:
- output 1: bfloat16 [8, 640, 2432], P('rep'), parts along dimension 0
- output 2: bfloat16 [8, 640, 2432], P('rep'), parts along dimension 0
- output 3: bfloat16 [8, 2432, 640], P('rep'), parts along dimension 0
- output 4: float32 [8, 640, 2432], P('rep'), parts along dimension 0
- output 5: float32 [8, 640, 2432], P('rep'), parts along dimension 0
- output 6: float32 [8, 2432, 640], P('rep'), parts along dimension 0
- output 7: float32 [8, 640, 2432], P('rep'), parts along dimension 0
- output 8: float32 [8, 640, 2432], P('rep'), parts along dimension 0
- output 9: float32 [8, 2432, 640], P('rep'), parts along dimension 0
There are 4 independent parts. A program takes and returns all parts, laid end to end along the dimension named above; an argument that names none is the same for every part.
All inputs are finite; a program needn't handle non-finite values.
Results may differ from a plain program's by a relative error of at most 0.022.
Values are sent between devices in bfloat16 or wider.
A program may use at most 2.5 GiB of HBM per device.

v0:
```python
import jax
import jax.numpy as jnp
from jax import lax
from jax.sharding import PartitionSpec as P

NAMES = ("w_gate", "w_up", "w_down")


def matmul(a, w):
    return jnp.dot(a, w, preferred_element_type=jnp.float32).astype(jnp.bfloat16)


def normed(h):
    wide = h.astype(jnp.float32)
    scale = lax.rsqrt(jnp.mean(wide**2, -1, keepdims=True) + 1e-6)
    return (wide * scale).astype(jnp.bfloat16)


def layer(h, w):
    a = normed(h)
    gate = jnp.dot(a, w["w_gate"], preferred_element_type=jnp.float32)
    up = jnp.dot(a, w["w_up"], preferred_element_type=jnp.float32)
    return h + matmul((jax.nn.silu(gate) * up).astype(jnp.bfloat16), w["w_down"])


def adamw(w, m, v, g):
    m = 0.9 * m + 0.1 * g
    v = 0.95 * v + 0.05 * g * g
    step = m * lax.rsqrt(v + 1e-8) + 0.1 * w
    return (w - 0.02 * step).astype(jnp.bfloat16), m, v


def clipped(gradients, sum_of_squares, count):
    factor = jnp.minimum(1.0, 0.5 * lax.rsqrt(sum_of_squares / count + 1e-30))
    return [g * factor for g in gradients]


def solution(mesh):
    def step(x, dy, *arrays):
        weights, m, v = (arrays[i : i + 3] for i in (0, 3, 6))
        layers = weights[0].shape[0]
        h, kept = x[0], []
        for number in range(layers):
            kept.append(h)
            h = layer(h, {name: w[number] for name, w in zip(NAMES, weights, strict=True)})
        by_h, summed = dy[0], [None] * layers
        for number in reversed(range(layers)):
            _, back = jax.vjp(lambda w, h: layer(h, w), {name: w[number] for name, w in zip(NAMES, weights, strict=True)}, kept[number])
            by_w, by_h = back(by_h)
            summed[number] = [lax.psum(by_w[name], "dp") for name in NAMES]
        gradients = [jnp.stack([summed[number][i] for number in range(layers)]).astype(jnp.float32) for i in range(3)]
        gradients = clipped(gradients, sum(jnp.sum(g * g) for g in gradients), sum(g.size for g in gradients))
        new = [adamw(w.astype(jnp.float32), m, v, g) for w, m, v, g in zip(weights, m, v, gradients, strict=True)]
        return tuple(one[which] for which in range(3) for one in new)

    return jax.shard_map(
        step,
        mesh=mesh,
        in_specs=(P(("rep", "dp"), None, None),) * 2 + (P(None, None, None),) * 9,
        out_specs=(P("rep", None, None),) * 9,
        check_vma=False,
    )
```

profile of v0, /device:TPU:0, one launch (start us, length us, event | category | flops | bytes accessed | tf_op | source)
XLA Modules:
  0.0 716.0 jit_solution(12884643233709033465)
XLA Ops:
  7.2 0.0 all-reduce.3.cloned.1.call-start
  7.2 3.0 copy.20
  10.2 0.6 fusion.36
  10.8 4.7 copy.21
  15.5 13.1 %convolution_convert_fusion.1 = bf16[2048,2432]{1,0:T(8,128)(2,1)} fusion(bf16[2,2432,640]{2,1,0:T(8,128)(2,1)} %param.15, bf16[1,2048,640]{2,1,0:T(8,128)(2,1)} %param.12), kind=kOutput, calls=%fused_computation.59 | convolution fusion | flops 6380322816 | bytes 15695872 | tf_op jit(solution)/shard_map/transpose(jvp())/dot_general | solution.py:10
  28.6 13.7 %fusion.70 = f32[2048,2432]{1,0:T(8,128)} fusion(bf16[2,640,2432]{2,1,0:T(8,128)(2,1)} %param.13, bf16[1,2048,640]{2,1,0:T(8,128)(2,1)S(1)} %copy-done.8, f32[2048]{0:T(1024)S(1)} %add_rsqrt_fusion), kind=kOutput, calls=%fused_computation.106 | convolution fusion | flops 6379274240 | bytes 25665536 | tf_op jit(solution)/shard_map/dot_general | solution.py:21
  42.3 19.5 %multiply_convert_fusion.1 = (bf16[2048,2432]{1,0:T(8,128)(2,1)}, f32[2048,2432]{1,0:T(8,128)}) fusion(f32[2048,2432]{1,0:T(8,128)} %fusion.70, bf16[2,640,2432]{2,1,0:T(8,128)(2,1)} %param.14, bf16[1,2048,640]{2,1,0:T(8,128)(2,1)} %param.11, f32[2048]{0:T(1024)S(1)} %add_rsqrt_fusion), kind=kOutput, calls=%fused_computation.17 | convolution fusion | flops 6409158656 | bytes 55549952 | tf_op jit(solution)/shard_map/dot_general | solution.py:22
  61.8 11.1 %fusion.40 = (f32[2048]{0:T(1024)S(1)}, bf16[2048,640]{0,1:T(8,128)(2,1)S(1)}) fusion(bf16[2048,2432]{1,0:T(8,128)(2,1)} %get-tuple-element.24, bf16[2,2432,640]{2,1,0:T(8,128)(2,1)} %param.15, bf16[1,2048,640]{1,2,0:T(8,128)(2,1)S(1)} %copy.20), kind=kOutput, calls=%fused_computation.76 | convolution fusion | flops 6381893632 | bytes 18325504 | tf_op jit(solution)/shard_map/dot_general | solution.py:10
  72.9 0.0 copy-start.9
  73.0 0.6 copy-done.9
  73.5 13.5 %fusion.59 = f32[2048,2432]{1,0:T(8,128)} fusion(bf16[2,640,2432]{2,1,0:T(8,128)(2,1)} %param.14, bf16[2048,640]{0,1:T(8,128)(2,1)S(1)} %get-tuple-element.27, f32[2048]{0:T(1024)S(1)} %fusion.98), kind=kOutput, calls=%fused_computation.95 | convolution fusion | flops 6379274240 | bytes 25665536 | tf_op jit(solution)/shard_map/jvp()/dot_general | solution.py:22
  87.0 26.9 %fusion.2 = (bf16[2048,2432]{1,0:T(8,128)(2,1)}, f32[2048,2432]{1,0:T(8,128)}) fusion(f32[2048,2432]{1,0:T(8,128)} %fusion.59, bf16[2048,2432]{1,0:T(8,128)(2,1)} %convolution_convert_fusion.1, bf16[2,640,2432]{2,1,0:T(8,128)(2,1)} %param.13, bf16[2048,640]{0,1:T(8,128)(2,1)S(1)} %get-tuple-element.27, f32[2048]{0:T(1024)S(1)} %fusion.98), kind=kOutput, calls=%fused_computation.8 | convolution fusion | flops 6439043072 | bytes 65511424 | tf_op jit(solution)/shard_map/jvp()/dot_general | solution.py:21
  113.9 14.9 %fusion.58 = bf16[2048,640]{0,1:T(8,128)(2,1)} fusion(bf16[2048,2432]{1,0:T(8,128)(2,1)} %convolution_convert_fusion.1, bf16[2,640,2432]{2,1,0:T(8,128)(2,1)S(1)} %bitcast.75, f32[2048,2432]{1,0:T(8,128)} %get-tuple-element.29), kind=kOutput, calls=%fused_computation.92 | convolution fusion | flops 6406537216 | bytes 35618816 | tf_op jit(solution)/shard_map/transpose(jvp())/dot_general | solution.py:22
  128.8 19.2 %fusion.56 = bf16[1,2432,640]{2,1,0:T(8,128)(2,1)} fusion(f32[2048,2432]{1,0:T(8,128)} %fusion.59, bf16[1,2048,640]{2,1,0:T(8,128)(2,1)} %param.12, f32[2048,2432]{1,0:T(8,128)} %get-tuple-element.29), kind=kOutput, calls=%fused_computation.91 | convolution fusion | flops 6406782976 | bytes 45580288 | tf_op jit(solution)/shard_map/transpose(jvp())/dot_general | solution.py:10
  148.1 0.0 slice-start.5
  148.1 11.5 %fusion.42 = (f32[2048]{0:T(1024)S(1)}, bf16[2048,640]{0,1:T(8,128)(2,1)S(1)}) fusion(bf16[2048,640]{0,1:T(8,128)(2,1)S(1)} %copy-done.7, bf16[2048,640]{0,1:T(8,128)(2,1)} %fusion.58, bf16[2048,2432]{1,0:T(8,128)(2,1)} %get-tuple-element.28, bf16[2,640,2432]{2,1,0:T(8,128)(2,1)} %param.13), kind=kOutput, calls=%fused_computation.78 | convolution fusion | flops 6381893632 | bytes 20946944 | tf_op jit(solution)/shard_map/transpose(jvp())/dot_general | solution.py:21
  159.6 0.0 slice-start.2
  159.7 1.8 fusion.82
  161.5 0.0 slice-start.3
  161.5 9.8 %fusion.50 = bf16[1,2432,640]{2,1,0:T(8,128)(2,1)} fusion(bf16[2048,2432]{1,0:T(8,128)(2,1)S(1)} %bitcast.79, bf16[2048,640]{0,1:T(8,128)(2,1)S(1)} %fusion.82), kind=kOutput, calls=%fused_computation.87 | convolution fusion | flops 6376898560 | bytes 15695872 | tf_op jit(solution)/shard_map/transpose(jvp())/dot_general | solution.py:10
  171.3 10.9 %convolution_convert_fusion = bf16[2048,2432]{1,0:T(8,128)(2,1)} fusion(bf16[2048,640]{0,1:T(8,128)(2,1)S(1)} %fusion.82, bf16[2,2432,640]{2,1,0:T(8,128)(2,1)S(1)} %bitcast.77), kind=kOutput, calls=%fused_computation.58 | convolution fusion | flops 6380322816 | bytes 15695872 | tf_op jit(solution)/shard_map/transpose(jvp())/dot_general | solution.py:10
  182.2 14.9 %fusion.52 = bf16[1,640,2432]{2,1,0:T(8,128)(2,1)} fusion(bf16[2048,2432]{1,0:T(8,128)(2,1)} %convolution_convert_fusion.1, bf16[2048,640]{0,1:T(8,128)(2,1)S(1)} %copy-done.7, f32[2048]{0:T(1024)S(1)} %fusion.98, f32[2048,2432]{1,0:T(8,128)} %get-tuple-element.29), kind=kOutput, calls=%fused_computation.89 | convolution fusion | flops 6410715136 | bytes 35627008 | tf_op jit(solution)/shard_map/transpose(jvp())/dot_general | solution.py:22
  197.1 12.2 %fusion.49 = bf16[1,640,2432]{2,1,0:T(8,128)(2,1)} fusion(bf16[2048,2432]{1,0:T(8,128)(2,1)} %get-tuple-element.28, bf16[2048,640]{0,1:T(8,128)(2,1)S(1)} %copy-done.7, f32[2048]{0:T(1024)S(1)} %fusion.98), kind=kOutput, calls=%fused_computation.86 | convolution fusion | flops 6379274240 | bytes 15704064 | tf_op jit(solution)/shard_map/transpose(jvp())/dot_general | solution.py:21
  209.4 14.7 %fusion.51 = bf16[1,640,2432]{2,1,0:T(8,128)(2,1)} fusion(bf16[2048,2432]{1,0:T(8,128)(2,1)} %convolution_convert_fusion, f32[2048,2432]{1,0:T(8,128)} %fusion.70, bf16[1,2048,640]{1,2,0:T(8,128)(2,1)S(1)} %copy-done.5, f32[2048]{0:T(1024)S(1)} %copy-done.12), kind=kOutput, calls=%fused_computation.88 | convolution fusion | flops 6410715136 | bytes 35627008 | tf_op jit(solution)/shard_map/transpose(jvp())/dot_general | solution.py:22
  224.1 20.8 %fusion.53 = bf16[1,640,2432]{2,1,0:T(8,128)(2,1)} fusion(f32[2048,2432]{1,0:T(8,128)} %fusion.70, f32[2048,2432]{1,0:T(8,128)} %get-tuple-element.25, bf16[2048,2432]{1,0:T(8,128)(2,1)} %convolution_convert_fusion, bf16[1,2048,640]{1,2,0:T(8,128)(2,1)S(1)} %copy-done.5, f32[2048]{0:T(1024)S(1)} %copy-done.12), kind=kOutput, calls=%fused_computation.90 | convolution fusion | flops 6435618816 | bytes 55549952 | tf_op jit(solution)/shard_map/transpose(jvp())/dot_general | solution.py:21
  244.9 0.0 all-reduce.3.cloned.1.call-update
  244.9 372.2 %all-reduce.3.cloned.1.call-done = (bf16[1,640,2432]{2,1,0:T(8,128)(2,1)}, bf16[1,640,2432]{2,1,0:T(8,128)(2,1)}, bf16[1,640,2432]{2,1,0:T(8,128)(2,1)}, bf16[1,...) async-done(((bf16[1,640,2432]{2,1,0:T(8,128)(2,1)}, bf16[1,640,2432]{2,1,0:T(8,128)(2,1)}, bf16[1,640,2432]{2,1,0:T(8,128)(2,1)}, ...) | async-done | bytes 18677776 | tf_op jit(solution)/shard_map/psum | solution.py:50
  617.2 6.8 fusion.24
  624.0 6.6 fusion.23
  630.6 3.8 fusion.22
  636.4 25.2 %fusion.30 = (bf16[2,2432,640]{2,1,0:T(8,128)(2,1)}, f32[2,2432,640]{2,1,0:T(8,128)}, f32[2,2432,640]{2,1,0:T(8,128)}) fusion(bf16[2,2432,640]{2,1,0:T(8,128)(2,1)} %param.15, f32[]{:T(128)S(6)} %min_shard_map.3, bf16[1,2432,640]{2,1,0:T(8,128)(2,1)S(1)} %copy-done, bf16[1,2432,640]{2,1,0:T(8,128)(2,1)} %get-tuple-element.14, f32[2,2432,640]{2,1,0:T(8,128)} %param.21, ...), kind=kLoop, calls=%fused_computation.54 | loop fusion | flops 62259200 | bytes 68485120 | tf_op jit(solution)/shard_map/convert_element_type | solution.py:30
  661.6 47.1 %fusion.21 = (bf16[2,640,2432]{2,1,0:T(8,128)(2,1)}, f32[2,640,2432]{2,1,0:T(8,128)}, f32[2,640,2432]{2,1,0:T(8,128)}, bf16[2,640,2432]{2,1,0:T(8,128)(2,1)}, f3...) fusion(bf16[2,640,2432]{2,1,0:T(8,128)(2,1)} %param.13, f32[]{:T(128)S(6)} %min_shard_map.3, ...), kind=kLoop, calls=%fused_computation.45 | loop fusion | flops 124518400 | bytes 136970240 | tf_op jit(solution)/shard_map/convert_element_type | solution.py:30
  (41 shorter events, 0.1 us)
Async XLA Ops:
  7.2 610.0 %all-reduce.3.cloned.1.call-start = ((), (), s32[]{:S(2)}) async-start(), calls=%async_computation | async-start | bytes 37355520 | tf_op jit(solution)/shard_map/psum | solution.py:50
  10.2 51.6 %copy-start.4 = (bf16[1,2048,640]{1,2,0:T(8,128)(2,1)}, bf16[1,2048,640]{1,2,0:T(8,128)(2,1)S(1)}, u32[]{:S(2)}) copy-start(bf16[1,2048,640]{1,2,0:T(8,128)(2,1)S(1)} %copy.20) | copy-start | bytes 7864324
  10.8 31.5 %copy-start.11 = (f32[2048]{0:T(1024)}, f32[2048]{0:T(1024)S(1)}, u32[]{:S(2)}) copy-start(f32[2048]{0:T(1024)S(1)} %add_rsqrt_fusion) | copy-start | bytes 24580
  15.5 13.1 %copy-start.8 = (bf16[1,2048,640]{2,1,0:T(8,128)(2,1)S(1)}, bf16[1,2048,640]{2,1,0:T(8,128)(2,1)}, u32[]{:S(2)}) copy-start(bf16[1,2048,640]{2,1,0:T(8,128)(2,1)} %param.11) | copy-start | bytes 7864324
  72.9 0.6 copy-start.9
  72.9 14.1 %copy-start.6 = (bf16[2048,640]{0,1:T(8,128)(2,1)}, bf16[2048,640]{0,1:T(8,128)(2,1)S(1)}, u32[]{:S(2)}) copy-start(bf16[2048,640]{0,1:T(8,128)(2,1)S(1)} %get-tuple-element.27) | copy-start | bytes 7864324
  73.5 40.4 %slice-start = ((s8[6225920]{0:T(1024)(128)(4,1)}), s8[4194304]{0:T(1024)(128)(4,1)S(1)}, s32[]{:S(2)}) async-start(s8[6225920]{0:T(1024)(128)(4,1)} %bitcast.74), calls=%async_computation.1 | async-start | bytes 8388608
  87.0 26.9 %slice-start.1 = ((s8[6225920]{0:T(1024)(128)(4,1)}), s8[2031616]{0:T(1024)(128)(4,1)S(1)}, s32[]{:S(2)}) async-start(s8[6225920]{0:T(1024)(128)(4,1)} %bitcast.74), calls=%async_computation.2 | async-start | bytes 4063232
  128.8 19.3 %copy-start.7 = (bf16[2048,640]{0,1:T(8,128)(2,1)S(1)}, bf16[2048,640]{0,1:T(8,128)(2,1)}, u32[]{:S(2)}) copy-start(bf16[2048,640]{0,1:T(8,128)(2,1)} %copy-done.6) | copy-start | bytes 7864324
  148.1 13.4 %slice-start.4 = ((s8[9961472]{0:T(1024)(128)(4,1)}), s8[4194304]{0:T(1024)(128)(4,1)S(1)}, s32[]{:S(2)}) async-start(s8[9961472]{0:T(1024)(128)(4,1)} %bitcast.78), calls=%async_computation.5 | async-start | bytes 8388608
  148.1 11.5 %copy-start.10 = (f32[2048]{0:T(1024)S(1)}, f32[2048]{0:T(1024)}, u32[]{:S(2)}) copy-start(f32[2048]{0:T(1024)} %copy-done.9) | copy-start | bytes 24580
  148.1 11.6 %copy-start.3 = (bf16[1,2048,640]{1,2,0:T(8,128)(2,1)S(1)}, bf16[1,2048,640]{1,2,0:T(8,128)(2,1)}, u32[]{:S(2)}) copy-start(bf16[1,2048,640]{1,2,0:T(8,128)(2,1)} %copy.21) | copy-start | bytes 7864324
  148.1 13.4 %slice-start.5 = ((s8[9961472]{0:T(1024)(128)(4,1)}), s8[4194304]{0:T(1024)(128)(4,1)S(1)}, s32[]{:S(2)}) async-start(s8[9961472]{0:T(1024)(128)(4,1)} %bitcast.78), calls=%async_computation.6 | async-start | bytes 8388608
  148.1 13.4 %slice-start.6 = ((s8[9961472]{0:T(1024)(128)(4,1)}), s8[1572864]{0:T(1024)(128)(4,1)S(1)}, s32[]{:S(2)}) async-start(s8[9961472]{0:T(1024)(128)(4,1)} %bitcast.78), calls=%async_computation.7 | async-start | bytes 3145728
  159.6 11.7 %slice-start.2 = ((s8[6225920]{0:T(1024)(128)(4,1)}), s8[4194304]{0:T(1024)(128)(4,1)S(1)}, s32[]{:S(2)}) async-start(s8[6225920]{0:T(1024)(128)(4,1)} %bitcast.76), calls=%async_computation.3 | async-start | bytes 8388608
  161.5 9.8 %slice-start.3 = ((s8[6225920]{0:T(1024)(128)(4,1)}), s8[2031616]{0:T(1024)(128)(4,1)S(1)}, s32[]{:S(2)}) async-start(s8[6225920]{0:T(1024)(128)(4,1)} %bitcast.76), calls=%async_computation.4 | async-start | bytes 4063232
  197.1 12.2 %copy-start.5 = (bf16[1,2048,640]{1,2,0:T(8,128)(2,1)S(1)}, bf16[1,2048,640]{1,2,0:T(8,128)(2,1)}, u32[]{:S(2)}) copy-start(bf16[1,2048,640]{1,2,0:T(8,128)(2,1)} %copy-done.4) | copy-start | bytes 7864324
  197.1 12.2 %copy-start.12 = (f32[2048]{0:T(1024)S(1)}, f32[2048]{0:T(1024)}, u32[]{:S(2)}) copy-start(f32[2048]{0:T(1024)} %copy-done.11) | copy-start | bytes 24580
  617.2 13.4 %copy-start.1 = (bf16[1,640,2432]{2,1,0:T(8,128)(2,1)S(1)}, bf16[1,640,2432]{2,1,0:T(8,128)(2,1)}, u32[]{:S(2)}) copy-start(bf16[1,640,2432]{2,1,0:T(8,128)(2,1)} %get-tuple-element.9) | copy-start | bytes 9338884
  617.2 13.4 %copy-start.2 = (bf16[1,640,2432]{2,1,0:T(8,128)(2,1)S(1)}, bf16[1,640,2432]{2,1,0:T(8,128)(2,1)}, u32[]{:S(2)}) copy-start(bf16[1,640,2432]{2,1,0:T(8,128)(2,1)} %get-tuple-element.10) | copy-start | bytes 9338884
  617.2 19.2 %copy-start = (bf16[1,2432,640]{2,1,0:T(8,128)(2,1)S(1)}, bf16[1,2432,640]{2,1,0:T(8,128)(2,1)}, u32[]{:S(2)}) copy-start(bf16[1,2432,640]{2,1,0:T(8,128)(2,1)} %get-tuple-element.13) | copy-start | bytes 9338884
Sparse Core Ops, SparseCore 0:
  245.1 372.0 all-reduce.2
where the time goes:
time: 724 us; the launch traced here: 716 us
  waiting for transfers between devices  372 us (51%)
  matrix products  227 us (31%)
  other arithmetic  91.8 us (13%)
  between operations  16.7 us (2%)
  local copies, waits for them, and re-layouts  8.36 us (1%)
    psum x1, waiting for transfers between devices, step(): summed[number] = [lax.psum(by_w[name], 'dp') for name in NAMES]  372 us
    dot_general x5, matrix products, layer(): gate = jnp.dot(a, w['w_gate'], preferred_element_type=jnp.float32)  85.2 us
    dot_general x5, matrix products, layer(): up = jnp.dot(a, w['w_up'], preferred_element_type=jnp.float32)  77.5 us
    convert_element_type x2, other arithmetic, adamw(): return ((w - 0.02 * step).astype(jnp.bfloat16), m, v)  72.2 us
    dot_general x5, matrix products, matmul(): jnp.dot(a, w, preferred_element_type=jnp.float32).astype(jnp.bfloat16)  64.1 us
    reduce_sum x3, other arithmetic, step(): jnp.sum(g * g)  17.2 us
  transfers between devices with their start and end apart: 1, of which 1 were waited for; matrix products, arithmetic and copies ran while one was open for 0% of the time, Pallas kernels for 0%

commit v1 on v0

v1 whole, which is shorter than its diff:
```python
import functools

import jax
import jax.numpy as jnp
from jax import lax
from jax.experimental import pallas as pl
from jax.experimental.pallas import tpu as pltpu
from jax.sharding import PartitionSpec as P

F32, BF16 = jnp.float32, jnp.bfloat16
MESH = pl.DeviceIdType.MESH
T, D, FF = 2048, 640, 2432
TILE = 256
STEPS = 10
LANES = 128
PER_LAYER = FF // LANES
UNITS = 2 * PER_LAYER
ROWS = 512
HALF, QUARTER = D // 2, D // 4
KEEP = 10
SLOTS = 4
LAG = 2
LAST = 2 * 2 * STEPS + 2 + 3 * LAG


def dot(a, b):
    return jnp.dot(a, b, preferred_element_type=F32)


def dot_t(a, b):
    return lax.dot_general(a, b, (((1,), (1,)), ((), ())), preferred_element_type=F32)


def norm_scale(h):
    wide = h.astype(F32)
    return wide, lax.rsqrt(jnp.mean(wide * wide, -1, keepdims=True) + 1e-6)


def gradient_kernel(
    x_hbm, dy_hbm, wg_hbm, wu_hbm, wd_hbm, g_hbm, ss_out,
    X, A, AT, H, DY, DYT, ACC, DT, ACT, WGU, WD, OWN, PART, UP, OUT, SQ, SS,
    sem_in, sem_w, sem_d2d, sem_part, sem_up, sem_out, sem_g, sem_gsend, sem_gd2d, sem_gpart, sem_ss, sem_sssend,
):
    rep, dp = lax.axis_index("rep"), lax.axis_index("dp")
    z, core = lax.div(dp, 2), lax.rem(dp, 2)

    def at(z, core):
        return (rep, z * 2 + core)

    partner = at(z, 1 - core)
    barrier = pltpu.get_barrier_semaphore()
    for other in range(1, 8):
        pl.semaphore_signal(barrier, inc=1, device_id=(rep, lax.rem(dp + other, 8)), device_id_type=MESH)

    x_copy = pltpu.make_async_copy(x_hbm.at[0], X, sem_in.at[0])
    dy_copy = pltpu.make_async_copy(dy_hbm.at[0], DY, sem_in.at[1])
    x_copy.start()

    def tile_copies(q, n):
        layer = jnp.where((q >= STEPS) & (q < 2 * STEPS), 1, 0)
        slot = lax.rem(q, 2)
        columns = pl.ds(pl.multiple_of(lax.rem(q, STEPS) * TILE, LANES), n)
        return (
            pltpu.make_async_copy(wg_hbm.at[layer, :, columns], WGU.at[slot, :, pl.ds(0, n)], sem_w.at[slot, 0]),
            pltpu.make_async_copy(wu_hbm.at[layer, :, columns], WGU.at[slot, :, pl.ds(TILE, n)], sem_w.at[slot, 1]),
            pltpu.make_async_copy(wd_hbm.at[layer, columns, :], WD.at[slot, pl.ds(0, n), :], sem_w.at[slot, 2]),
        )

    def load(q):
        short = lax.rem(q, STEPS) == STEPS - 1
        slot = lax.rem(q, 2)

        @pl.when(jnp.logical_not(short))
        def _():
            for copy in tile_copies(q, TILE):
                copy.start()

        @pl.when(short)
        def _():
            WGU[slot, :, LANES:TILE] = jnp.zeros((D, LANES), BF16)
            WGU[slot, :, TILE + LANES :] = jnp.zeros((D, LANES), BF16)
            WD[slot, LANES:, :] = jnp.zeros((LANES, D), BF16)
            for copy in tile_copies(q, LANES):
                copy.start()

    def wait_tile(q):
        short = lax.rem(q, STEPS) == STEPS - 1

        @pl.when(jnp.logical_not(short))
        def _():
            for copy in tile_copies(q, TILE):
                copy.wait()

        @pl.when(short)
        def _():
            for copy in tile_copies(q, LANES):
                copy.wait()

    load(jnp.int32(0))
    dy_copy.start()
    x_copy.wait()
    block = 256

    def rows_of(r):
        return pl.ds(pl.multiple_of(r * block, block), block)

    @pl.loop(0, T // block)
    def _(r):
        rows = rows_of(r)
        wide, scale = norm_scale(X[rows, :])
        A[rows, :] = (wide * scale).astype(BF16)

    def forward(q, first):
        slot = lax.rem(q, 2)
        wait_tile(q)
        load(q + 1)
        for r in range(0, T, ROWS):
            gu = dot(A[r : r + ROWS, :], WGU[slot])
            g, u = gu[:, :TILE], gu[:, TILE:]
            sig = 0.5 * jnp.tanh(0.5 * g) + 0.5
            h = dot((g * sig * u).astype(BF16), WD[slot])
            if first:
                ACC[r : r + ROWS, :] = h
            else:
                ACC[r : r + ROWS, :] += h

    forward(jnp.int32(0), True)

    @pl.loop(1, STEPS)
    def _(q):
        forward(q, False)

    dy_copy.wait()

    @pl.loop(0, T // block)
    def _(r):
        rows = rows_of(r)
        h = (X[rows, :].astype(F32) + ACC[rows, :].astype(BF16).astype(F32)).astype(BF16)
        H[rows, :] = h
        wide, scale = norm_scale(h)
        a = (wide * scale).astype(BF16)
        A[rows, :] = a
        AT[:, rows] = a.T
        DYT[:, rows] = DY[rows, :].T

    pl.semaphore_wait(barrier, 7)

    def next_layer():
        @pl.loop(0, T // block)
        def _(r):
            rows = rows_of(r)
            h, scale = norm_scale(H[rows, :])
            da = ACC[rows, :].astype(BF16).astype(F32)
            along = jnp.mean(da * h, -1, keepdims=True) * scale * scale
            dh = (scale * (da - h * along)).astype(BF16)
            d = (DY[rows, :].astype(F32) + dh.astype(F32)).astype(BF16)
            DY[rows, :] = d
            DYT[:, rows] = d.T
            wide, scale = norm_scale(X[rows, :])
            a = (wide * scale).astype(BF16)
            A[rows, :] = a
            AT[:, rows] = a.T

    SQ[...] = jnp.zeros_like(SQ)

    def exists(v):
        return (v >= 0) & (v < 4 * STEPS) & (lax.rem(v, 2 * STEPS) != 2 * STEPS - 1)

    def packed(v):
        return v - jnp.where(v >= 2 * STEPS, 1, 0)

    def part_copy(v):
        w = packed(v)
        return pltpu.make_async_remote_copy(
            src_ref=OWN.at[lax.rem(v, KEEP), :, pl.ds(pl.multiple_of((1 - core) * HALF, 16), HALF), :],
            dst_ref=PART.at[w],
            send_sem=sem_d2d.at[lax.rem(v, 4)],
            recv_sem=sem_part.at[w],
            device_id=partner,
            device_id_type=MESH,
        )

    def my_rows(way):
        return pl.ds(pl.multiple_of(core * HALF + way * QUARTER, 16), QUARTER)

    def up_copy(way, w):
        return pltpu.make_async_remote_copy(
            src_ref=OUT.at[way, lax.rem(w, SLOTS)],
            dst_ref=UP.at[way, w],
            send_sem=sem_out.at[way, lax.rem(w, SLOTS)],
            recv_sem=sem_up.at[way, w],
            device_id=at(jnp.clip(z - 1, 0, 3) if way == 0 else jnp.clip(z + 1, 0, 3), core),
            device_id_type=MESH,
        )

    def keep_copy(way, w):
        return pltpu.make_async_copy(
            OUT.at[way, lax.rem(w, SLOTS)], g_hbm.at[w, :, my_rows(way), :], sem_out.at[way, lax.rem(w, SLOTS)]
        )

    def reduce(way, v):
        starts, ends = (z == 3, z == 0) if way == 0 else (z == 0, z == 3)
        comes_first = (z >= 2) if way == 0 else (z < 2)

        @pl.when(exists(v))
        def _():
            w = packed(v)
            slot = lax.rem(w, SLOTS)

            @pl.when(comes_first)
            def _():
                part_copy(v).wait_recv()

            @pl.when(w >= SLOTS)
            def _():
                keep_copy(way, w).wait()

            rows = pl.ds(way * QUARTER, QUARTER)

            def two(k):
                own = OWN[lax.rem(v, KEEP), k, my_rows(way), :].astype(F32)
                return own + PART[w, k, rows, :].astype(F32)

            @pl.when(starts)
            def _():
                for k in range(3):
                    OUT[way, slot, k] = two(k).astype(BF16)

            @pl.when(jnp.logical_not(starts))
            def _():
                up_copy(way, w).wait_recv()
                for k in range(3):
                    OUT[way, slot, k] = (two(k) + UP[way, w, k].astype(F32)).astype(BF16)

            @pl.when(jnp.logical_not(ends))
            def _():
                up_copy(way, w).start()

            @pl.when(ends)
            def _():
                keep_copy(way, w).start()
                total = jnp.zeros((8, LANES), F32)
                for k in range(3):
                    g = OUT[way, slot, k].astype(F32)
                    total += jnp.sum((g * g).reshape(QUARTER // 8, 8, LANES), 0)
                SQ[...] += total

    def communicate(n):
        reduce(0, n - 2 - LAG * (3 - z))
        reduce(1, n - 2 - LAG * z)

    @pl.loop(0, 2 * STEPS)
    def _(t):
        q = t + STEPS
        slot = lax.rem(q, 2)

        @pl.when(t == STEPS)
        def _():
            next_layer()

        wait_tile(q)

        @pl.when(q < 3 * STEPS - 1)
        def _():
            load(q + 1)

        for r in range(0, T, ROWS):
            gu = dot(A[r : r + ROWS, :], WGU[slot])
            da = dot_t(DY[r : r + ROWS, :], WD[slot]).astype(BF16).astype(F32)
            g, u = gu[:, :TILE], gu[:, TILE:]
            sig = 0.5 * jnp.tanh(0.5 * g) + 0.5
            s = g * sig
            ACT[r : r + ROWS, :] = (s * u).astype(BF16)
            DT[r : r + ROWS, TILE:] = (da * s).astype(BF16)
            DT[r : r + ROWS, :TILE] = (da * u * (sig + s * (1.0 - sig))).astype(BF16)

        communicate(2 * t)

        keep = lax.rem(t, KEEP // 2) * 2
        dgu = dot(AT[...], DT[...]).astype(BF16)
        for k in range(2):
            for half in range(2):
                OWN[keep + half, k] = dgu[:, k * TILE + half * LANES : k * TILE + (half + 1) * LANES]
        dd = dot(DYT[...], ACT[...]).astype(BF16)
        for half in range(2):
            OWN[keep + half, 2] = dd[:, half * LANES : (half + 1) * LANES]

        for half in range(2):
            v = 2 * t + half

            @pl.when(exists(v - 2))
            def _():
                part_copy(v - 2).wait_send()

            @pl.when(exists(v))
            def _():
                part_copy(v).start()

        @pl.when(t == 0)
        def _():
            ACC[...] = jnp.zeros_like(ACC)

        @pl.when(t < STEPS)
        def _():
            for r in range(0, T, ROWS):
                ACC[r : r + ROWS, :] += dot_t(DT[r : r + ROWS, :], WGU[slot])

        communicate(2 * t + 1)

    part_copy(jnp.int32(4 * STEPS - 2)).wait_send()

    @pl.loop(4 * STEPS, LAST)
    def _(n):
        communicate(n)

    for way in range(2):
        for w in range(UNITS - SLOTS, UNITS):
            keep_copy(way, jnp.int32(w)).wait()

    mine = jnp.where(z == 3, 2, 0) + core
    holds = (z == 0) | (z == 3)

    def ss_copy(other):
        return pltpu.make_async_remote_copy(
            src_ref=SQ,
            dst_ref=SS.at[mine],
            send_sem=sem_sssend.at[other],
            recv_sem=sem_ss.at[mine],
            device_id=(rep, lax.rem(dp + other, 8)),
            device_id_type=MESH,
        )

    @pl.when(holds)
    def _():
        for other in range(1, 8):
            ss_copy(other).start()
        SS[mine] = SQ[...]

    def g_rows(way, w):
        return g_hbm.at[w, :, my_rows(way), :]

    def forward_copy(way, w):
        return pltpu.make_async_remote_copy(
            src_ref=g_rows(way, w),
            dst_ref=g_rows(way, w),
            send_sem=sem_gsend.at[way],
            recv_sem=sem_g.at[way, w],
            device_id=at(jnp.clip(z + 1, 0, 3) if way == 0 else jnp.clip(z - 1, 0, 3), core),
            device_id_type=MESH,
        )

    def share_copy(way, w):
        return pltpu.make_async_remote_copy(
            src_ref=g_rows(way, w),
            dst_ref=g_rows(way, w),
            send_sem=sem_gd2d.at[way],
            recv_sem=sem_gpart.at[way],
            device_id=partner,
            device_id_type=MESH,
        )

    @pl.loop(0, UNITS + 6)
    def _(n):
        for way in range(2):
            distance = z if way == 0 else 3 - z
            w = n - 2 * distance

            @pl.when((w >= 0) & (w < UNITS))
            def _():
                @pl.when(distance > 0)
                def _():
                    forward_copy(way, w).wait_recv()

                @pl.when(distance < 3)
                def _():
                    forward_copy(way, w).start()

                share_copy(way, w).start()

    for way in range(2):
        theirs = pl.ds(pl.multiple_of((1 - core) * HALF + way * QUARTER, 16), QUARTER)
        everything = g_hbm.at[:, :, my_rows(way), :]
        others = g_hbm.at[:, :, theirs, :]

        @pl.when((z < 3) if way == 0 else (z > 0))
        def _():
            pltpu.make_async_copy(everything, everything, sem_gsend.at[way]).wait()

        pltpu.make_async_copy(everything, everything, sem_gd2d.at[way]).wait()
        pltpu.make_async_copy(others, others, sem_gpart.at[way]).wait()

    for piece in range(4):

        @pl.when(jnp.logical_not(holds & (mine == piece)))
        def _():
            pltpu.make_async_copy(SS.at[piece], SS.at[piece], sem_ss.at[piece]).wait()

    @pl.when(holds)
    def _():
        for other in range(1, 8):
            ss_copy(other).wait_send()

    ss_out[...] = (SS[0] + SS[1]) + (SS[2] + SS[3])


def gradients(x, dy, w_gate, w_up, w_down):
    hbm = pl.BlockSpec(memory_space=pl.ANY)

    def vmem(*shape):
        return pltpu.VMEM(shape, BF16)

    dma = pltpu.SemaphoreType.DMA
    return pl.pallas_call(
        gradient_kernel,
        out_shape=(
            jax.ShapeDtypeStruct((UNITS, 3, D, LANES), BF16),
            jax.ShapeDtypeStruct((8, LANES), F32),
        ),
        in_specs=[hbm] * 5,
        out_specs=(hbm, pl.BlockSpec(memory_space=pltpu.VMEM)),
        scratch_shapes=[
            vmem(T, D), vmem(T, D), vmem(D, T), vmem(T, D), vmem(T, D), vmem(D, T),
            pltpu.VMEM((T, D), F32),
            vmem(T, 2 * TILE), vmem(T, TILE), vmem(2, D, 2 * TILE), vmem(2, TILE, D),
            vmem(KEEP, 3, D, LANES), vmem(UNITS, 3, HALF, LANES), vmem(2, UNITS, 3, QUARTER, LANES),
            vmem(2, SLOTS, 3, QUARTER, LANES),
            pltpu.VMEM((8, LANES), F32), pltpu.VMEM((4, 8, LANES), F32),
            dma((2,)), dma((2, 3)), dma((4,)), dma((UNITS,)), dma((2, UNITS)), dma((2, SLOTS)),
            dma((2, UNITS)), dma((2,)), dma((2,)), dma((2,)), dma((4,)), dma((8,)),
        ],
        compiler_params=pltpu.CompilerParams(collective_id=0, has_side_effects=True, vmem_limit_bytes=63 * 2**20),
        name="gradients",
    )(x, dy, w_gate, w_up, w_down)


def update(w, m, v, g):
    m = 0.9 * m + 0.1 * g
    v = 0.95 * v + 0.05 * g * g
    step = m * lax.rsqrt(v + 1e-8) + 0.1 * w
    return (w - 0.02 * step).astype(BF16), m, v


def clip_factor(ss_ref):
    total = jnp.sum(ss_ref[...], keepdims=True)
    return jnp.minimum(1.0, 0.5 * lax.rsqrt(total / (UNITS * 3 * D * LANES) + 1e-30))


def rows_kernel(ss, g, w, m, v, w_out, m_out, v_out):
    factor = clip_factor(ss)
    for unit in range(PER_LAYER):
        at = (0, slice(None), slice(unit * LANES, (unit + 1) * LANES))
        new = update(w[at].astype(F32), m[at], v[at], g[unit, 0].astype(F32) * factor)
        w_out[at], m_out[at], v_out[at] = new


def columns_kernel(ss, g, w, m, v, w_out, m_out, v_out):
    factor = clip_factor(ss)
    gradient = g[0, 0].astype(F32).T * factor
    w_out[0], m_out[0], v_out[0] = update(w[0].astype(F32), m[0], v[0], gradient)


def adamw(which, ss, g, w, m, v):
    if which < 2:
        rows = 64
        grid = (2, D // rows)
        kernel = rows_kernel
        g_spec = pl.BlockSpec((PER_LAYER, 1, rows, LANES), lambda layer, i: (1 - layer, which, i, 0))
        spec = pl.BlockSpec((1, rows, FF), lambda layer, i: (layer, i, 0))
    else:
        grid = (2, PER_LAYER)
        kernel = columns_kernel
        g_spec = pl.BlockSpec((1, 1, D, LANES), lambda layer, i: ((1 - layer) * PER_LAYER + i, 2, 0, 0))
        spec = pl.BlockSpec((1, LANES, D), lambda layer, i: (layer, i, 0))
    return pl.pallas_call(
        kernel,
        grid=grid,
        in_specs=[pl.BlockSpec((8, LANES), lambda layer, i: (0, 0)), g_spec, spec, spec, spec],
        out_specs=(spec, spec, spec),
        out_shape=(
            jax.ShapeDtypeStruct(w.shape, BF16),
            jax.ShapeDtypeStruct(w.shape, F32),
            jax.ShapeDtypeStruct(w.shape, F32),
        ),
        compiler_params=pltpu.CompilerParams(vmem_limit_bytes=48 * 2**20),
        name=f"adamw_{which}",
    )(ss, g, w, m, v)


def solution(mesh):
    def step(x, dy, *arrays):
        weights, m, v = (arrays[i : i + 3] for i in (0, 3, 6))
        g, ss = gradients(x, dy, *weights)
        new = [adamw(which, ss, g, weights[which], m[which], v[which]) for which in range(3)]
        return tuple(one[which] for which in range(3) for one in new)

    return jax.shard_map(
        step,
        mesh=mesh,
        in_specs=(P(("rep", "dp"), None, None),) * 2 + (P(None, None, None),) * 9,
        out_specs=(P("rep", None, None),) * 9,
        check_vma=False,
    )
```

time: 724 us -> 404 us (0.56)
  Pallas kernels: 0 us -> 401 us
  waiting for transfers between devices: 372 us -> 0 us
  matrix products: 227 us -> 0 us
  other arithmetic: 91.8 us -> 0 us
  between operations: 16.7 us -> 0.66 us
  local copies, waits for them, and re-layouts: 8.36 us -> 0.68 us
    pallas_call x0 -> x4, Pallas kernels: none -> 401 us  [the longest x1 300 us: gradients(): pl.pallas_call(gradient_kernel, out_shape=(jax.ShapeDtypeStruct((UNITS, 3...]
    psum x1 -> x0, waiting for transfers between devices: 372 us -> none  [step(): summed[number] = [lax.psum(by_w[name], 'dp') for name in NAMES]]
    dot_general x15 -> x0, matrix products: 227 us -> none  [the longest x5 85.2 us: layer(): gate = jnp.dot(a, w['w_gate'], preferred_element_type=jnp.float32)]
    convert_element_type x2 -> x0, other arithmetic: 72.2 us -> none  [adamw(): return ((w - 0.02 * step).astype(jnp.bfloat16), m, v)]
    reduce_sum x4 -> x0, other arithmetic: 17.8 us -> none  [the longest x3 17.2 us: step(): jnp.sum(g * g)]
    unnamed x42 -> x2, local copies, waits for them, and re-layouts: 8.36 us -> 0.68 us
  transfers between devices with their start and end apart: 1 -> 0, of which waited for: 1 -> 0; matrix products, arithmetic and copies ran while one was open for 0% -> 0% of each run, Pallas kernels for 0% -> 0%
where the time goes in v1:
time: 404 us; the launch traced here: 402 us
  Pallas kernels  401 us (99%)
    pallas_call x1, Pallas kernels, gradients(): pl.pallas_call(gradient_kernel, out_shape=(jax.ShapeDtypeStruct((UNITS, 3...  300 us
    pallas_call x3, Pallas kernels, adamw(): pl.pallas_call(kernel, grid=grid, in_specs=[pl.BlockSpec((8, LANES), lamb...  101 us

profile of v1, /device:TPU:0, one launch (start us, length us, event | category | flops | bytes accessed | tf_op | source)
XLA Modules:
  0.0 401.9 jit_solution(8859454101257879778)
XLA Ops:
  0.6 299.6 %gradients.1 = (bf16[38,3,640,128]{3,2,1,0:T(8,128)(2,1)}, f32[8,128]{1,0:T(8,128)}) custom-call(bf16[1,2048,640]{2,1,0:T(8,128)(2,1)} %x_hbm.1, bf16[1,2048,640]{2,1,0:T(8,128)(2,1)} %dy_hbm.1, bf16[2,640,2432]{2,1,0:T(8,128)(2,1)} %w.3, bf16[2,640,2432]{2,1,0:T(8,128)(2,1)} %w.4, bf16[2,2432,640]{2,1,0:T(8,128)(2,1)} %w.5), custom_call_target="tpu_custom_call" | custom-call | tf_op jit(solution)/shard_map/gradients/pallas_call | solution.py:413
  300.3 0.0 copy-start
  300.3 0.7 copy-done
  301.0 41.8 %adamw_2.1 = (bf16[2,2432,640]{2,1,0:T(8,128)(2,1)}, f32[2,2432,640]{2,1,0:T(8,128)}, f32[2,2432,640]{2,1,0:T(8,128)}) custom-call(f32[8,128]{1,0:T(8,128)S(1)} %copy-done, bf16[38,3,640,128]{3,2,1,0:T(8,128)(2,1)} %get-tuple-element.21.g, bf16[2,2432,640]{2,1,0:T(8,128)(2,1)} %w.5, f32[2,2432,640]{2,1,0:T(8,128)} %m.5, f32[2,2432,640]{2,1,0:T(8,128)} %v.5), custom_call_target="tpu_custom_call" | custom-call | tf_op jit(solution)/shard_map/adamw_2/pallas_call | solution.py:474
  342.8 29.6 %adamw_1.1 = (bf16[2,640,2432]{2,1,0:T(8,128)(2,1)}, f32[2,640,2432]{2,1,0:T(8,128)}, f32[2,640,2432]{2,1,0:T(8,128)}) custom-call(f32[8,128]{1,0:T(8,128)S(1)} %copy-done, bf16[38,3,640,128]{3,2,1,0:T(8,128)(2,1)} %get-tuple-element.21.g, bf16[2,640,2432]{2,1,0:T(8,128)(2,1)} %w.4, f32[2,640,2432]{2,1,0:T(8,128)} %m.4, f32[2,640,2432]{2,1,0:T(8,128)} %v.4), custom_call_target="tpu_custom_call" | custom-call | tf_op jit(solution)/shard_map/adamw_1/pallas_call | solution.py:474
  372.4 29.6 %adamw_0.1 = (bf16[2,640,2432]{2,1,0:T(8,128)(2,1)}, f32[2,640,2432]{2,1,0:T(8,128)}, f32[2,640,2432]{2,1,0:T(8,128)}) custom-call(f32[8,128]{1,0:T(8,128)S(1)} %copy-done, bf16[38,3,640,128]{3,2,1,0:T(8,128)(2,1)} %get-tuple-element.21.g, bf16[2,640,2432]{2,1,0:T(8,128)(2,1)} %w.3, f32[2,640,2432]{2,1,0:T(8,128)} %m.3, f32[2,640,2432]{2,1,0:T(8,128)} %v.3), custom_call_target="tpu_custom_call" | custom-call | tf_op jit(solution)/shard_map/adamw_0/pallas_call | solution.py:474
Async XLA Ops:
  300.3 0.7 copy-start

commit v2 on v1

--- a/solution.py
+++ b/solution.py
@@ -16,11 +16,14 @@
 PER_LAYER = FF // LANES
 UNITS = 2 * PER_LAYER
 ROWS = 512
-HALF, QUARTER = D // 2, D // 4
+HALF = D // 2
 KEEP = 10
 SLOTS = 4
 LAG = 2
 LAST = 2 * 2 * STEPS + 2 + 3 * LAG
+EARLY, RATE = 14, 1
+
+DEEP, AHEAD = 6, 3
 
 
 def dot(a, b):
@@ -162,6 +165,11 @@
             AT[:, rows] = a.T
 
     SQ[...] = jnp.zeros_like(SQ)
+    distance = jnp.where(core == 0, 3 - z, z)
+    onward = jnp.where(core == 0, jnp.maximum(z - 1, 0), jnp.minimum(z + 1, 3))
+    back = jnp.where(core == 0, jnp.minimum(z + 1, 3), jnp.maximum(z - 1, 0))
+    mine = pl.ds(pl.multiple_of(core * HALF, 16), HALF)
+    theirs = pl.ds(pl.multiple_of((1 - core) * HALF, 16), HALF)
 
     def exists(v):
         return (v >= 0) & (v < 4 * STEPS) & (lax.rem(v, 2 * STEPS) != 2 * STEPS - 1)
@@ -172,7 +180,7 @@
     def part_copy(v):
         w = packed(v)
         return pltpu.make_async_remote_copy(
-            src_ref=OWN.at[lax.rem(v, KEEP), :, pl.ds(pl.multiple_of((1 - core) * HALF, 16), HALF), :],
+            src_ref=OWN.at[lax.rem(v, KEEP), :, theirs, :],
             dst_ref=PART.at[w],
             send_sem=sem_d2d.at[lax.rem(v, 4)],
             recv_sem=sem_part.at[w],
@@ -180,74 +188,98 @@
             device_id_type=MESH,
         )
 
-    def my_rows(way):
-        return pl.ds(pl.multiple_of(core * HALF + way * QUARTER, 16), QUARTER)
-
-    def up_copy(way, w):
+    def up_copy(w):
         return pltpu.make_async_remote_copy(
-            src_ref=OUT.at[way, lax.rem(w, SLOTS)],
-            dst_ref=UP.at[way, w],
-            send_sem=sem_out.at[way, lax.rem(w, SLOTS)],
-            recv_sem=sem_up.at[way, w],
-            device_id=at(jnp.clip(z - 1, 0, 3) if way == 0 else jnp.clip(z + 1, 0, 3), core),
+            src_ref=OUT.at[lax.rem(w, SLOTS)],
+            dst_ref=UP.at[w],
+            send_sem=sem_out.at[lax.rem(w, SLOTS)],
+            recv_sem=sem_up.at[w],
+            device_id=at(onward, core),
             device_id_type=MESH,
         )
 
-    def keep_copy(way, w):
-        return pltpu.make_async_copy(
-            OUT.at[way, lax.rem(w, SLOTS)], g_hbm.at[w, :, my_rows(way), :], sem_out.at[way, lax.rem(w, SLOTS)]
-        )
-
-    def reduce(way, v):
-        starts, ends = (z == 3, z == 0) if way == 0 else (z == 0, z == 3)
-        comes_first = (z >= 2) if way == 0 else (z < 2)
-
+    def keep_copy(w):
+        return pltpu.make_async_copy(OUT.at[lax.rem(w, SLOTS)], g_hbm.at[w, :, mine, :], sem_out.at[lax.rem(w, SLOTS)])
+
+    def reduce(v):
         @pl.when(exists(v))
         def _():
             w = packed(v)
             slot = lax.rem(w, SLOTS)
-
-            @pl.when(comes_first)
-            def _():
-                part_copy(v).wait_recv()
+            part_copy(v).wait_recv()
 
             @pl.when(w >= SLOTS)
             def _():
-                keep_copy(way, w).wait()
-
-            rows = pl.ds(way * QUARTER, QUARTER)
+                keep_copy(w).wait()
 
             def two(k):
-                own = OWN[lax.rem(v, KEEP), k, my_rows(way), :].astype(F32)
-                return own + PART[w, k, rows, :].astype(F32)
-
-            @pl.when(starts)
+                return OWN[lax.rem(v, KEEP), k, mine, :].astype(F32) + PART[w, k].astype(F32)
+
+            @pl.when(distance == 0)
             def _():
                 for k in range(3):
-                    OUT[way, slot, k] = two(k).astype(BF16)
-
-            @pl.when(jnp.logical_not(starts))
-            def _():
-                up_copy(way, w).wait_recv()
+                    OUT[slot, k] = two(k).astype(BF16)
+
+            @pl.when(distance > 0)
+            def _():
+                up_copy(w).wait_recv()
                 for k in range(3):
-                    OUT[way, slot, k] = (two(k) + UP[way, w, k].astype(F32)).astype(BF16)
-
-            @pl.when(jnp.logical_not(ends))
-            def _():
-                up_copy(way, w).start()
-
-            @pl.when(ends)
-            def _():
-                keep_copy(way, w).start()
+                    OUT[slot, k] = (two(k) + UP[w, k].astype(F32)).astype(BF16)
+
+            @pl.when(distance < 3)
+            def _():
+                up_copy(w).start()
+
+            @pl.when(distance == 3)
+            def _():
+                keep_copy(w).start()
                 total = jnp.zeros((8, LANES), F32)
                 for k in range(3):
-                    g = OUT[way, slot, k].astype(F32)
-                    total += jnp.sum((g * g).reshape(QUARTER // 8, 8, LANES), 0)
+                    g = OUT[slot, k].astype(F32)
+                    total += jnp.sum((g * g).reshape(HALF // 8, 8, LANES), 0)
                 SQ[...] += total
 
+    def back_copy(w):
+        return pltpu.make_async_remote_copy(
+            src_ref=g_hbm.at[w, :, mine, :],
+            dst_ref=g_hbm.at[w, :, mine, :],
+            send_sem=sem_gsend.at[0],
+            recv_sem=sem_g.at[w],
+            device_id=at(back, core),
+            device_id_type=MESH,
+        )
+
+    def share_copy(w):
+        return pltpu.make_async_remote_copy(
+            src_ref=g_hbm.at[w, :, mine, :],
+            dst_ref=g_hbm.at[w, :, mine, :],
+            send_sem=sem_gd2d.at[0],
+            recv_sem=sem_gpart.at[0],
+            device_id=partner,
+            device_id_type=MESH,
+        )
+
+    def gather(n):
+        w = n - (3 - distance)
+
+        @pl.when((w >= 0) & (w < UNITS))
+        def _():
+            @pl.when(distance < 3)
+            def _():
+                back_copy(w).wait_recv()
+
+            @pl.when(distance > 0)
+            def _():
+                back_copy(w).start()
+
+            share_copy(w).start()
+
     def communicate(n):
-        reduce(0, n - 2 - LAG * (3 - z))
-        reduce(1, n - 2 - LAG * z)
+        reduce(n - 2 - LAG * distance)
+
+        @pl.when((n >= EARLY) & (lax.rem(n - EARLY, RATE) == 0))
+        def _():
+            gather(lax.div(n - EARLY, RATE))
 
     @pl.loop(0, 2 * STEPS)
     def _(t):
@@ -313,94 +345,51 @@
     def _(n):
         communicate(n)
 
-    for way in range(2):
-        for w in range(UNITS - SLOTS, UNITS):
-            keep_copy(way, jnp.int32(w)).wait()
-
-    mine = jnp.where(z == 3, 2, 0) + core
-    holds = (z == 0) | (z == 3)
+    for w in range(UNITS - SLOTS, UNITS):
+        keep_copy(jnp.int32(w)).wait()
 
     def ss_copy(other):
         return pltpu.make_async_remote_copy(
             src_ref=SQ,
-            dst_ref=SS.at[mine],
+            dst_ref=SS.at[core],
             send_sem=sem_sssend.at[other],
-            recv_sem=sem_ss.at[mine],
+            recv_sem=sem_ss.at[core],
             device_id=(rep, lax.rem(dp + other, 8)),
             device_id_type=MESH,
         )
 
-    @pl.when(holds)
+    @pl.when(distance == 3)
     def _():
         for other in range(1, 8):
             ss_copy(other).start()
-        SS[mine] = SQ[...]
-
-    def g_rows(way, w):
-        return g_hbm.at[w, :, my_rows(way), :]
-
-    def forward_copy(way, w):
-        return pltpu.make_async_remote_copy(
-            src_ref=g_rows(way, w),
-            dst_ref=g_rows(way, w),
-            send_sem=sem_gsend.at[way],
-            recv_sem=sem_g.at[way, w],
-            device_id=at(jnp.clip(z + 1, 0, 3) if way == 0 else jnp.clip(z - 1, 0, 3), core),
-            device_id_type=MESH,
-        )
-
-    def share_copy(way, w):
-        return pltpu.make_async_remote_copy(
-            src_ref=g_rows(way, w),
-            dst_ref=g_rows(way, w),
-            send_sem=sem_gd2d.at[way],
-            recv_sem=sem_gpart.at[way],
-            device_id=partner,
-            device_id_type=MESH,
-        )
-
-    @pl.loop(0, UNITS + 6)
+        SS[core] = SQ[...]
+
+    @pl.loop((LAST - EARLY + RATE - 1) // RATE, UNITS + 3)
     def _(n):
-        for way in range(2):
-            distance = z if way == 0 else 3 - z
-            w = n - 2 * distance
-
-            @pl.when((w >= 0) & (w < UNITS))
-            def _():
-                @pl.when(distance > 0)
-                def _():
-                    forward_copy(way, w).wait_recv()
-
-                @pl.when(distance < 3)
-                def _():
-                    forward_copy(way, w).start()
-
-                share_copy(way, w).start()
-
-    for way in range(2):
-        theirs = pl.ds(pl.multiple_of((1 - core) * HALF + way * QUARTER, 16), QUARTER)
-        everything = g_hbm.at[:, :, my_rows(way), :]
-        others = g_hbm.at[:, :, theirs, :]
-
-        @pl.when((z < 3) if way == 0 else (z > 0))
-        def _():
-            pltpu.make_async_copy(everything, everything, sem_gsend.at[way]).wait()
-
-        pltpu.make_async_copy(everything, everything, sem_gd2d.at[way]).wait()
-        pltpu.make_async_copy(others, others, sem_gpart.at[way]).wait()
-
-    for piece in range(4):
-
-        @pl.when(jnp.logical_not(holds & (mine == piece)))
+        gather(n)
+
+    everything = g_hbm.at[:, :, mine, :]
+    others = g_hbm.at[:, :, theirs, :]
+
+    @pl.when(distance > 0)
+    def _():
+        pltpu.make_async_copy(everything, everything, sem_gsend.at[0]).wait()
+
+    pltpu.make_async_copy(everything, everything, sem_gd2d.at[0]).wait()
+    pltpu.make_async_copy(others, others, sem_gpart.at[0]).wait()
+
+    for piece in range(2):
+
+        @pl.when(jnp.logical_not((distance == 3) & (core == piece)))
         def _():
             pltpu.make_async_copy(SS.at[piece], SS.at[piece], sem_ss.at[piece]).wait()
 
-    @pl.when(holds)
+    @pl.when(distance == 3)
     def _():
         for other in range(1, 8):
             ss_copy(other).wait_send()
 
-    ss_out[...] = (SS[0] + SS[1]) + (SS[2] + SS[3])
+    ss_out[...] = SS[0] + SS[1]
 
 
 def gradients(x, dy, w_gate, w_up, w_down):
@@ -422,11 +411,10 @@
             vmem(T, D), vmem(T, D), vmem(D, T), vmem(T, D), vmem(T, D), vmem(D, T),
             pltpu.VMEM((T, D), F32),
             vmem(T, 2 * TILE), vmem(T, TILE), vmem(2, D, 2 * TILE), vmem(2, TILE, D),
-            vmem(KEEP, 3, D, LANES), vmem(UNITS, 3, HALF, LANES), vmem(2, UNITS, 3, QUARTER, LANES),
-            vmem(2, SLOTS, 3, QUARTER, LANES),
-            pltpu.VMEM((8, LANES), F32), pltpu.VMEM((4, 8, LANES), F32),
-            dma((2,)), dma((2, 3)), dma((4,)), dma((UNITS,)), dma((2, UNITS)), dma((2, SLOTS)),
-            dma((2, UNITS)), dma((2,)), dma((2,)), dma((2,)), dma((4,)), dma((8,)),
+            vmem(KEEP, 3, D, LANES), vmem(UNITS, 3, HALF, LANES), vmem(UNITS, 3, HALF, LANES), vmem(SLOTS, 3, HALF, LANES),
+            pltpu.VMEM((8, LANES), F32), pltpu.VMEM((2, 8, LANES), F32),
+            dma((2,)), dma((2, 3)), dma((4,)), dma((UNITS,)), dma((UNITS,)), dma((SLOTS,)),
+            dma((UNITS,)), dma((1,)), dma((1,)), dma((1,)), dma((2,)), dma((8,)),
         ],
         compiler_params=pltpu.CompilerParams(collective_id=0, has_side_effects=True, vmem_limit_bytes=63 * 2**20),
         name="gradients",
@@ -445,53 +433,99 @@
     return jnp.minimum(1.0, 0.5 * lax.rsqrt(total / (UNITS * 3 * D * LANES) + 1e-30))
 
 
-def rows_kernel(ss, g, w, m, v, w_out, m_out, v_out):
+def adamw_kernel(ss, g, *refs):
+    w_in, m_in, v_in, w_new, m_new, v_new = (refs[i : i + 3] for i in range(0, 18, 3))
+    WI, MI, VI, GI, WO, DWI, DMI, DVI, DWO, sem_in, sem_out = refs[18:]
     factor = clip_factor(ss)
-    for unit in range(PER_LAYER):
-        at = (0, slice(None), slice(unit * LANES, (unit + 1) * LANES))
-        new = update(w[at].astype(F32), m[at], v[at], g[unit, 0].astype(F32) * factor)
-        w_out[at], m_out[at], v_out[at] = new
-
-
-def columns_kernel(ss, g, w, m, v, w_out, m_out, v_out):
-    factor = clip_factor(ss)
-    gradient = g[0, 0].astype(F32).T * factor
-    w_out[0], m_out[0], v_out[0] = update(w[0].astype(F32), m[0], v[0], gradient)
-
-
-def adamw(which, ss, g, w, m, v):
-    if which < 2:
-        rows = 64
-        grid = (2, D // rows)
-        kernel = rows_kernel
-        g_spec = pl.BlockSpec((PER_LAYER, 1, rows, LANES), lambda layer, i: (1 - layer, which, i, 0))
-        spec = pl.BlockSpec((1, rows, FF), lambda layer, i: (layer, i, 0))
-    else:
-        grid = (2, PER_LAYER)
-        kernel = columns_kernel
-        g_spec = pl.BlockSpec((1, 1, D, LANES), lambda layer, i: ((1 - layer) * PER_LAYER + i, 2, 0, 0))
-        spec = pl.BlockSpec((1, LANES, D), lambda layer, i: (layer, i, 0))
+
+    def place(k, u):
+        columns = pl.ds(pl.multiple_of(lax.rem(u, PER_LAYER) * LANES, LANES), LANES)
+        layer = jnp.where(u < PER_LAYER, 1, 0)
+        return (layer, slice(None), columns) if k < 2 else (layer, columns, slice(None))
+
+    def buffers(k, u):
+        slot = lax.rem(u, DEEP)
+        if k < 2:
+            return tuple(ref.at[slot, k] for ref in (WI, MI, VI, WO))
+        return tuple(ref.at[slot] for ref in (DWI, DMI, DVI, DWO))
+
+    def reads(k, u):
+        slot, at, (w, m, v, _) = lax.rem(u, DEEP), place(k, u), buffers(k, u)
+        pairs = ((w_in[k].at[at], w), (m_in[k].at[at], m), (v_in[k].at[at], v), (g.at[u, k], GI.at[slot, k]))
+        return [pltpu.make_async_copy(src, dst, sem_in.at[slot, k, i]) for i, (src, dst) in enumerate(pairs)]
+
+    def writes(k, u):
+        slot, at, (_, m, v, w) = lax.rem(u, DEEP), place(k, u), buffers(k, u)
+        pairs = ((w, w_new[k].at[at]), (m, m_new[k].at[at]), (v, v_new[k].at[at]))
+        return [pltpu.make_async_copy(src, dst, sem_out.at[slot, k, i]) for i, (src, dst) in enumerate(pairs)]
+
+    def start_reads(u):
+        for k in range(3):
+            for copy in reads(k, u):
+                copy.start()
+
+    for u in range(AHEAD):
+        start_reads(jnp.int32(u))
+
+    @pl.loop(0, UNITS)
+    def _(u):
+        slot = lax.rem(u, DEEP)
+        later = u + AHEAD
+
+        @pl.when(later < UNITS)
+        def _():
+            @pl.when(later >= DEEP)
+            def _():
+                for k in range(3):
+                    for copy in writes(k, later - DEEP):
+                        copy.wait()
+
+            start_reads(later)
+
+        for k in range(3):
+            for copy in reads(k, u):
+                copy.wait()
+            w, m, v, out = buffers(k, u)
+            step = 160 if k < 2 else LANES
+            for r in range(0, D, step):
+                piece = slice(r, r + step)
+                gradient = GI[slot, k, piece, :]
+                at = (piece, slice(None)) if k < 2 else (slice(None), piece)
+                gradient = (gradient if k < 2 else gradient.T).astype(F32) * factor
+                out[at], m[at], v[at] = update(w[at].astype(F32), m[at], v[at], gradient)
+            for copy in writes(k, u):
+                copy.start()
+
+    for u in range(UNITS - DEEP, UNITS):
+        for k in range(3):
+            for copy in writes(k, jnp.int32(u)):
+                copy.wait()
+
+
+def adamw(ss, g, weights, m, v):
+    hbm = pl.BlockSpec(memory_space=pl.ANY)
+    dma = pltpu.SemaphoreType.DMA
     return pl.pallas_call(
-        kernel,
-        grid=grid,
-        in_specs=[pl.BlockSpec((8, LANES), lambda layer, i: (0, 0)), g_spec, spec, spec, spec],
-        out_specs=(spec, spec, spec),
-        out_shape=(
-            jax.ShapeDtypeStruct(w.shape, BF16),
-            jax.ShapeDtypeStruct(w.shape, F32),
-            jax.ShapeDtypeStruct(w.shape, F32),
-        ),
-        compiler_params=pltpu.CompilerParams(vmem_limit_bytes=48 * 2**20),
-        name=f"adamw_{which}",
-    )(ss, g, w, m, v)
+        adamw_kernel,
+        in_specs=[pl.BlockSpec(memory_space=pltpu.VMEM)] + [hbm] * 10,
+        out_specs=(hbm,) * 9,
+        out_shape=tuple(jax.ShapeDtypeStruct(a.shape, a.dtype) for a in (*weights, *m, *v)),
+        scratch_shapes=[
+            pltpu.VMEM((DEEP, 2, D, LANES), BF16), pltpu.VMEM((DEEP, 2, D, LANES), F32), pltpu.VMEM((DEEP, 2, D, LANES), F32),
+            pltpu.VMEM((DEEP, 3, D, LANES), BF16), pltpu.VMEM((DEEP, 2, D, LANES), BF16),
+            pltpu.VMEM((DEEP, LANES, D), BF16), pltpu.VMEM((DEEP, LANES, D), F32), pltpu.VMEM((DEEP, LANES, D), F32),
+            pltpu.VMEM((DEEP, LANES, D), BF16), dma((DEEP, 3, 4)), dma((DEEP, 3, 3)),
+        ],
+        compiler_params=pltpu.CompilerParams(vmem_limit_bytes=60 * 2**20),
+        name="adamw",
+    )(ss, g, *weights, *m, *v)
 
 
 def solution(mesh):
     def step(x, dy, *arrays):
         weights, m, v = (arrays[i : i + 3] for i in (0, 3, 6))
         g, ss = gradients(x, dy, *weights)
-        new = [adamw(which, ss, g, weights[which], m[which], v[which]) for which in range(3)]
-        return tuple(one[which] for which in range(3) for one in new)
+        return adamw(ss, g, weights, m, v)
 
     return jax.shard_map(
         step,

time: 404 us -> 355 us (0.88)
  Pallas kernels: 401 us -> 354 us
    pallas_call x3 -> x1, Pallas kernels: 101 us -> 67.8 us  [adamw(): pl.pallas_call(adamw_kernel, in_specs=[pl.BlockSpec(memory_space=pltpu.VM...]
    pallas_call x1, Pallas kernels: 300 us -> 286 us  [gradients(): pl.pallas_call(gradient_kernel, out_shape=(jax.ShapeDtypeStruct((UNITS, 3...]
where the time goes in v2:
time: 355 us; the launch traced here: 354 us
  Pallas kernels  354 us (100%)
    pallas_call x1, Pallas kernels, gradients(): pl.pallas_call(gradient_kernel, out_shape=(jax.ShapeDtypeStruct((UNITS, 3...  286 us
    pallas_call x1, Pallas kernels, adamw(): pl.pallas_call(adamw_kernel, in_specs=[pl.BlockSpec(memory_space=pltpu.VM...  67.8 us

profile of v2, /device:TPU:0, one launch (start us, length us, event | category | flops | bytes accessed | tf_op | source)
XLA Modules:
  0.0 354.4 jit_solution(11719365974336789910)
XLA Ops:
  0.6 285.8 %gradients.1 = (bf16[38,3,640,128]{3,2,1,0:T(8,128)(2,1)}, f32[8,128]{1,0:T(8,128)}) custom-call(bf16[1,2048,640]{2,1,0:T(8,128)(2,1)} %x_hbm.1, bf16[1,2048,640]{2,1,0:T(8,128)(2,1)} %dy_hbm.1, bf16[2,640,2432]{2,1,0:T(8,128)(2,1)} %refs_0_.1, bf16[2,640,2432]{2,1,0:T(8,128)(2,1)} %refs_1_.1, bf16[2,2432,640]{2,1,0:T(8,128)(2,1)} %refs_2_.1), custom_call_target="tpu_custom_call" | custom-call | tf_op jit(solution)/shard_map/gradients/pallas_call | solution.py:402
  286.4 67.8 %adamw.1 = (bf16[2,640,2432]{2,1,0:T(8,128)(2,1)}, bf16[2,640,2432]{2,1,0:T(8,128)(2,1)}, bf16[2,2432,640]{2,1,0:T(8,128)(2,1)}, f32[2,640,2432]{2,1,0:T(8,128)}...) custom-call(f32[8,128]{1,0:T(8,128)} %get-tuple-element.11.ss, ...), custom_call_target="tpu_custom_call" | custom-call | tf_op jit(solution)/shard_map/adamw/pallas_call | solution.py:508

commit v3 on v2

--- a/solution.py
+++ b/solution.py
@@ -15,13 +15,15 @@
 LANES = 128
 PER_LAYER = FF // LANES
 UNITS = 2 * PER_LAYER
-ROWS = 512
+ROWS, FORWARD_ROWS = 512, 1024
 HALF = D // 2
 KEEP = 10
 SLOTS = 4
+FIRST = 1
 LAG = 2
-LAST = 2 * 2 * STEPS + 2 + 3 * LAG
-EARLY, RATE = 14, 1
+BACK = 2
+SUMMED = 2 * 2 * STEPS + FIRST + 3 * LAG
+LAST = SUMMED + 3 * BACK
 
 DEEP, AHEAD = 6, 3
 
@@ -40,9 +42,9 @@
 
 
 def gradient_kernel(
-    x_hbm, dy_hbm, wg_hbm, wu_hbm, wd_hbm, g_hbm, ss_out,
-    X, A, AT, H, DY, DYT, ACC, DT, ACT, WGU, WD, OWN, PART, UP, OUT, SQ, SS,
-    sem_in, sem_w, sem_d2d, sem_part, sem_up, sem_out, sem_g, sem_gsend, sem_gd2d, sem_gpart, sem_ss, sem_sssend,
+    x_hbm, dy_hbm, wg_hbm, wu_hbm, wd_hbm, G, ss_out,
+    X, A, AT, H, DY, DYT, ACC, DT, ACT, WGU, WD, OWN, PART, OUT, SQ, SS,
+    sem_in, sem_w, sem_d2d, sem_part, sem_up, sem_out, sem_g, sem_gsend, sem_share, sem_shared, sem_ss, sem_sssend,
 ):
     rep, dp = lax.axis_index("rep"), lax.axis_index("dp")
     z, core = lax.div(dp, 2), lax.rem(dp, 2)
@@ -55,9 +57,17 @@
     for other in range(1, 8):
         pl.semaphore_signal(barrier, inc=1, device_id=(rep, lax.rem(dp + other, 8)), device_id_type=MESH)
 
-    x_copy = pltpu.make_async_copy(x_hbm.at[0], X, sem_in.at[0])
-    dy_copy = pltpu.make_async_copy(dy_hbm.at[0], DY, sem_in.at[1])
-    x_copy.start()
+    block = 256
+
+    def rows_of(r):
+        return pl.ds(pl.multiple_of(r * block, block), block)
+
+    def x_copy(r):
+        return pltpu.make_async_copy(x_hbm.at[0, rows_of(r), :], X.at[rows_of(r), :], sem_in.at[r])
+
+    dy_copy = pltpu.make_async_copy(dy_hbm.at[0], DY, sem_in.at[T // block])
+    for r in range(T // block):
+        x_copy(jnp.int32(r)).start()
 
     def tile_copies(q, n):
         layer = jnp.where((q >= STEPS) & (q < 2 * STEPS), 1, 0)
@@ -101,14 +111,10 @@
 
     load(jnp.int32(0))
     dy_copy.start()
-    x_copy.wait()
-    block = 256
-
-    def rows_of(r):
-        return pl.ds(pl.multiple_of(r * block, block), block)
 
     @pl.loop(0, T // block)
     def _(r):
+        x_copy(r).wait()
         rows = rows_of(r)
         wide, scale = norm_scale(X[rows, :])
         A[rows, :] = (wide * scale).astype(BF16)
@@ -117,23 +123,25 @@
         slot = lax.rem(q, 2)
         wait_tile(q)
         load(q + 1)
-        for r in range(0, T, ROWS):
-            gu = dot(A[r : r + ROWS, :], WGU[slot])
+        for r in range(0, T, FORWARD_ROWS):
+            gu = dot(A[r : r + FORWARD_ROWS, :], WGU[slot])
             g, u = gu[:, :TILE], gu[:, TILE:]
             sig = 0.5 * jnp.tanh(0.5 * g) + 0.5
             h = dot((g * sig * u).astype(BF16), WD[slot])
             if first:
-                ACC[r : r + ROWS, :] = h
+                ACC[r : r + FORWARD_ROWS, :] = h
             else:
-                ACC[r : r + ROWS, :] += h
+                ACC[r : r + FORWARD_ROWS, :] += h
+        if not first:
+            rows = rows_of(jnp.minimum(q - 1, T // block - 1))
+            DYT[:, rows] = DY[rows, :].T
 
     forward(jnp.int32(0), True)
+    dy_copy.wait()
 
     @pl.loop(1, STEPS)
     def _(q):
         forward(q, False)
-
-    dy_copy.wait()
 
     @pl.loop(0, T // block)
     def _(r):
@@ -144,7 +152,6 @@
         a = (wide * scale).astype(BF16)
         A[rows, :] = a
         AT[:, rows] = a.T
-        DYT[:, rows] = DY[rows, :].T
 
     pl.semaphore_wait(barrier, 7)
 
@@ -191,58 +198,17 @@
     def up_copy(w):
         return pltpu.make_async_remote_copy(
             src_ref=OUT.at[lax.rem(w, SLOTS)],
-            dst_ref=UP.at[w],
+            dst_ref=G.at[w, :, mine, :],
             send_sem=sem_out.at[lax.rem(w, SLOTS)],
             recv_sem=sem_up.at[w],
             device_id=at(onward, core),
             device_id_type=MESH,
         )
 
-    def keep_copy(w):
-        return pltpu.make_async_copy(OUT.at[lax.rem(w, SLOTS)], g_hbm.at[w, :, mine, :], sem_out.at[lax.rem(w, SLOTS)])
-
-    def reduce(v):
-        @pl.when(exists(v))
-        def _():
-            w = packed(v)
-            slot = lax.rem(w, SLOTS)
-            part_copy(v).wait_recv()
-
-            @pl.when(w >= SLOTS)
-            def _():
-                keep_copy(w).wait()
-
-            def two(k):
-                return OWN[lax.rem(v, KEEP), k, mine, :].astype(F32) + PART[w, k].astype(F32)
-
-            @pl.when(distance == 0)
-            def _():
-                for k in range(3):
-                    OUT[slot, k] = two(k).astype(BF16)
-
-            @pl.when(distance > 0)
-            def _():
-                up_copy(w).wait_recv()
-                for k in range(3):
-                    OUT[slot, k] = (two(k) + UP[w, k].astype(F32)).astype(BF16)
-
-            @pl.when(distance < 3)
-            def _():
-                up_copy(w).start()
-
-            @pl.when(distance == 3)
-            def _():
-                keep_copy(w).start()
-                total = jnp.zeros((8, LANES), F32)
-                for k in range(3):
-                    g = OUT[slot, k].astype(F32)
-                    total += jnp.sum((g * g).reshape(HALF // 8, 8, LANES), 0)
-                SQ[...] += total
-
     def back_copy(w):
         return pltpu.make_async_remote_copy(
-            src_ref=g_hbm.at[w, :, mine, :],
-            dst_ref=g_hbm.at[w, :, mine, :],
+            src_ref=G.at[w, :, mine, :],
+            dst_ref=G.at[w, :, mine, :],
             send_sem=sem_gsend.at[0],
             recv_sem=sem_g.at[w],
             device_id=at(back, core),
@@ -251,22 +217,63 @@
 
     def share_copy(w):
         return pltpu.make_async_remote_copy(
-            src_ref=g_hbm.at[w, :, mine, :],
-            dst_ref=g_hbm.at[w, :, mine, :],
-            send_sem=sem_gd2d.at[0],
-            recv_sem=sem_gpart.at[0],
+            src_ref=G.at[w, :, mine, :],
+            dst_ref=G.at[w, :, mine, :],
+            send_sem=sem_share.at[0],
+            recv_sem=sem_shared.at[0],
             device_id=partner,
             device_id_type=MESH,
         )
 
-    def gather(n):
-        w = n - (3 - distance)
-
-        @pl.when((w >= 0) & (w < UNITS))
-        def _():
+    def reduce(v):
+        @pl.when(exists(v))
+        def _():
+            w = packed(v)
+            slot = lax.rem(w, SLOTS)
+            part_copy(v).wait_recv()
+
+            def two(k):
+                return OWN[lax.rem(v, KEEP), k, mine, :].astype(F32) + PART[w, k].astype(F32)
+
+            @pl.when((w >= SLOTS) & (distance < 3))
+            def _():
+                up_copy(w).wait_send()
+
+            @pl.when(distance == 0)
+            def _():
+                for k in range(3):
+                    OUT[slot, k] = two(k).astype(BF16)
+
+            @pl.when(distance > 0)
+            def _():
+                up_copy(w).wait_recv()
+
+            @pl.when((distance > 0) & (distance < 3))
+            def _():
+                for k in range(3):
+                    OUT[slot, k] = (two(k) + G[w, k, mine, :].astype(F32)).astype(BF16)
+
             @pl.when(distance < 3)
             def _():
-                back_copy(w).wait_recv()
+                up_copy(w).start()
+
+            @pl.when(distance == 3)
+            def _():
+                total = jnp.zeros((8, LANES), F32)
+                for k in range(3):
+                    g = (two(k) + G[w, k, mine, :].astype(F32)).astype(BF16)
+                    G[w, k, mine, :] = g
+                    g = g.astype(F32)
+                    total += jnp.sum((g * g).reshape(HALF // 8, 8, LANES), 0)
+                SQ[...] += total
+                back_copy(w).start()
+                share_copy(w).start()
+
+    def gather(v):
+        @pl.when(exists(v) & (distance < 3))
+        def _():
+            w = packed(v)
+            back_copy(w).wait_recv()
 
             @pl.when(distance > 0)
             def _():
@@ -274,12 +281,19 @@
 
             share_copy(w).start()
 
+    def ss_copy(other):
+        return pltpu.make_async_remote_copy(
+            src_ref=SQ,
+            dst_ref=SS.at[core],
+            send_sem=sem_sssend.at[other],
+            recv_sem=sem_ss.at[core],
+            device_id=(rep, lax.rem(dp + other, 8)),
+            device_id_type=MESH,
+        )
+
     def communicate(n):
-        reduce(n - 2 - LAG * distance)
-
-        @pl.when((n >= EARLY) & (lax.rem(n - EARLY, RATE) == 0))
-        def _():
-            gather(lax.div(n - EARLY, RATE))
+        reduce(n - FIRST - LAG * distance)
+        gather(n - FIRST - LAG * 3 - BACK * (3 - distance))
 
     @pl.loop(0, 2 * STEPS)
     def _(t):
@@ -345,38 +359,26 @@
     def _(n):
         communicate(n)
 
-    for w in range(UNITS - SLOTS, UNITS):
-        keep_copy(jnp.int32(w)).wait()
-
-    def ss_copy(other):
-        return pltpu.make_async_remote_copy(
-            src_ref=SQ,
-            dst_ref=SS.at[core],
-            send_sem=sem_sssend.at[other],
-            recv_sem=sem_ss.at[core],
-            device_id=(rep, lax.rem(dp + other, 8)),
-            device_id_type=MESH,
-        )
-
-    @pl.when(distance == 3)
+        @pl.when((n == SUMMED) & (distance == 3))
+        def _():
+            for other in range(1, 8):
+                ss_copy(other).start()
+            SS[core] = SQ[...]
+
+    @pl.when(distance < 3)
     def _():
-        for other in range(1, 8):
-            ss_copy(other).start()
-        SS[core] = SQ[...]
-
-    @pl.loop((LAST - EARLY + RATE - 1) // RATE, UNITS + 3)
-    def _(n):
-        gather(n)
-
-    everything = g_hbm.at[:, :, mine, :]
-    others = g_hbm.at[:, :, theirs, :]
+        for w in range(UNITS - SLOTS, UNITS):
+            up_copy(jnp.int32(w)).wait_send()
+
+    everything = G.at[:, :, mine, :]
+    others = G.at[:, :, theirs, :]
 
     @pl.when(distance > 0)
     def _():
         pltpu.make_async_copy(everything, everything, sem_gsend.at[0]).wait()
 
-    pltpu.make_async_copy(everything, everything, sem_gd2d.at[0]).wait()
-    pltpu.make_async_copy(others, others, sem_gpart.at[0]).wait()
+    pltpu.make_async_copy(everything, everything, sem_share.at[0]).wait()
+    pltpu.make_async_copy(others, others, sem_shared.at[0]).wait()
 
     for piece in range(2):
 
@@ -401,22 +403,19 @@
     dma = pltpu.SemaphoreType.DMA
     return pl.pallas_call(
         gradient_kernel,
-        out_shape=(
-            jax.ShapeDtypeStruct((UNITS, 3, D, LANES), BF16),
-            jax.ShapeDtypeStruct((8, LANES), F32),
-        ),
+        out_shape=(vmem(UNITS, 3, D, LANES), pltpu.VMEM((8, LANES), F32)),
         in_specs=[hbm] * 5,
-        out_specs=(hbm, pl.BlockSpec(memory_space=pltpu.VMEM)),
+        out_specs=(pl.BlockSpec(memory_space=pltpu.VMEM),) * 2,
         scratch_shapes=[
             vmem(T, D), vmem(T, D), vmem(D, T), vmem(T, D), vmem(T, D), vmem(D, T),
             pltpu.VMEM((T, D), F32),
             vmem(T, 2 * TILE), vmem(T, TILE), vmem(2, D, 2 * TILE), vmem(2, TILE, D),
-            vmem(KEEP, 3, D, LANES), vmem(UNITS, 3, HALF, LANES), vmem(UNITS, 3, HALF, LANES), vmem(SLOTS, 3, HALF, LANES),
+            vmem(KEEP, 3, D, LANES), vmem(UNITS, 3, HALF, LANES), vmem(SLOTS, 3, HALF, LANES),
             pltpu.VMEM((8, LANES), F32), pltpu.VMEM((2, 8, LANES), F32),
-            dma((2,)), dma((2, 3)), dma((4,)), dma((UNITS,)), dma((UNITS,)), dma((SLOTS,)),
+            dma((T // 256 + 1,)), dma((2, 3)), dma((4,)), dma((UNITS,)), dma((UNITS,)), dma((SLOTS,)),
             dma((UNITS,)), dma((1,)), dma((1,)), dma((1,)), dma((2,)), dma((8,)),
         ],
-        compiler_params=pltpu.CompilerParams(collective_id=0, has_side_effects=True, vmem_limit_bytes=63 * 2**20),
+        compiler_params=pltpu.CompilerParams(collective_id=0, has_side_effects=True, vmem_limit_bytes=46 * 2**20),
         name="gradients",
     )(x, dy, w_gate, w_up, w_down)
 
@@ -435,7 +434,7 @@
 
 def adamw_kernel(ss, g, *refs):
     w_in, m_in, v_in, w_new, m_new, v_new = (refs[i : i + 3] for i in range(0, 18, 3))
-    WI, MI, VI, GI, WO, DWI, DMI, DVI, DWO, sem_in, sem_out = refs[18:]
+    WI, MI, VI, WO, DWI, DMI, DVI, DWO, sem_in, sem_out = refs[18:]
     factor = clip_factor(ss)
 
     def place(k, u):
@@ -451,7 +450,7 @@
 
     def reads(k, u):
         slot, at, (w, m, v, _) = lax.rem(u, DEEP), place(k, u), buffers(k, u)
-        pairs = ((w_in[k].at[at], w), (m_in[k].at[at], m), (v_in[k].at[at], v), (g.at[u, k], GI.at[slot, k]))
+        pairs = ((w_in[k].at[at], w), (m_in[k].at[at], m), (v_in[k].at[at], v))
         return [pltpu.make_async_copy(src, dst, sem_in.at[slot, k, i]) for i, (src, dst) in enumerate(pairs)]
 
     def writes(k, u):
@@ -469,7 +468,6 @@
 
     @pl.loop(0, UNITS)
     def _(u):
-        slot = lax.rem(u, DEEP)
         later = u + AHEAD
 
         @pl.when(later < UNITS)
@@ -489,7 +487,7 @@
             step = 160 if k < 2 else LANES
             for r in range(0, D, step):
                 piece = slice(r, r + step)
-                gradient = GI[slot, k, piece, :]
+                gradient = g[u, k, piece, :]
                 at = (piece, slice(None)) if k < 2 else (slice(None), piece)
                 gradient = (gradient if k < 2 else gradient.T).astype(F32) * factor
                 out[at], m[at], v[at] = update(w[at].astype(F32), m[at], v[at], gradient)
@@ -503,20 +501,21 @@
 
 
 def adamw(ss, g, weights, m, v):
-    hbm = pl.BlockSpec(memory_space=pl.ANY)
+    hbm = pl.BlockSpec(memory_space=pltpu.HBM)
+    ss, g = (pltpu.with_memory_space_constraint(a, pltpu.VMEM) for a in (ss, g))
     dma = pltpu.SemaphoreType.DMA
     return pl.pallas_call(
         adamw_kernel,
-        in_specs=[pl.BlockSpec(memory_space=pltpu.VMEM)] + [hbm] * 10,
+        in_specs=[pl.BlockSpec(memory_space=pltpu.VMEM)] * 2 + [hbm] * 9,
         out_specs=(hbm,) * 9,
         out_shape=tuple(jax.ShapeDtypeStruct(a.shape, a.dtype) for a in (*weights, *m, *v)),
         scratch_shapes=[
             pltpu.VMEM((DEEP, 2, D, LANES), BF16), pltpu.VMEM((DEEP, 2, D, LANES), F32), pltpu.VMEM((DEEP, 2, D, LANES), F32),
-            pltpu.VMEM((DEEP, 3, D, LANES), BF16), pltpu.VMEM((DEEP, 2, D, LANES), BF16),
+            pltpu.VMEM((DEEP, 2, D, LANES), BF16),
             pltpu.VMEM((DEEP, LANES, D), BF16), pltpu.VMEM((DEEP, LANES, D), F32), pltpu.VMEM((DEEP, LANES, D), F32),
-            pltpu.VMEM((DEEP, LANES, D), BF16), dma((DEEP, 3, 4)), dma((DEEP, 3, 3)),
+            pltpu.VMEM((DEEP, LANES, D), BF16), dma((DEEP, 3, 3)), dma((DEEP, 3, 3)),
         ],
-        compiler_params=pltpu.CompilerParams(vmem_limit_bytes=60 * 2**20),
+        compiler_params=pltpu.CompilerParams(vmem_limit_bytes=46 * 2**20),
         name="adamw",
     )(ss, g, *weights, *m, *v)
 

time: 355 us -> 331 us (0.932)
  Pallas kernels: 354 us -> 331 us
    pallas_call x1, Pallas kernels: 286 us -> 270 us  [gradients(): pl.pallas_call(gradient_kernel, out_shape=(vmem(UNITS, 3, D, LANES), pltp...]
    pallas_call x1, Pallas kernels: 67.8 us -> 60.9 us  [adamw(): pl.pallas_call(adamw_kernel, in_specs=[pl.BlockSpec(memory_space=pltpu.VM...]
where the time goes in v3:
time: 331 us
  Pallas kernels  331 us (100%)
    pallas_call x1, Pallas kernels, gradients(): pl.pallas_call(gradient_kernel, out_shape=(vmem(UNITS, 3, D, LANES), pltp...  270 us
    pallas_call x1, Pallas kernels, adamw(): pl.pallas_call(adamw_kernel, in_specs=[pl.BlockSpec(memory_space=pltpu.VM...  60.9 us

profile of v3, /device:TPU:0, one launch (start us, length us, event | category | flops | bytes accessed | tf_op | source)
XLA Modules:
  0.0 331.3 jit_solution(9774671061196290480)
XLA Ops:
  0.6 269.7 %gradients.1 = (bf16[38,3,640,128]{3,2,1,0:T(8,128)(2,1)S(1)}, f32[8,128]{1,0:T(8,128)S(1)}) custom-call(bf16[1,2048,640]{2,1,0:T(8,128)(2,1)} %x_hbm.1, bf16[1,2048,640]{2,1,0:T(8,128)(2,1)} %dy_hbm.1, bf16[2,640,2432]{2,1,0:T(8,128)(2,1)} %refs_0_.1, bf16[2,640,2432]{2,1,0:T(8,128)(2,1)} %refs_1_.1, bf16[2,2432,640]{2,1,0:T(8,128)(2,1)} %refs_2_.1), custom_call_target="tpu_custom_call" | custom-call | tf_op jit(solution)/shard_map/gradients/pallas_call | solution.py:404
  270.4 60.9 %adamw.1 = (bf16[2,640,2432]{2,1,0:T(8,128)(2,1)}, bf16[2,640,2432]{2,1,0:T(8,128)(2,1)}, bf16[2,2432,640]{2,1,0:T(8,128)(2,1)}, f32[2,640,2432]{2,1,0:T(8,128)}...) custom-call(f32[8,128]{1,0:T(8,128)S(1)} %get-tuple-element.11.ss, ...), custom_call_target="tpu_custom_call" | custom-call | tf_op jit(solution)/shard_map/adamw/pallas_call | solution.py:507

commit v4 on v3

--- a/solution.py
+++ b/solution.py
@@ -24,8 +24,10 @@
 BACK = 2
 SUMMED = 2 * 2 * STEPS + FIRST + 3 * LAG
 LAST = SUMMED + 3 * BACK
+AT_A_TIME = -(-UNITS // (LAST - SUMMED))
 
 DEEP, AHEAD = 6, 3
+AHEAD_UNITS = T // LANES
 
 
 def dot(a, b):
@@ -42,10 +44,11 @@
 
 
 def gradient_kernel(
-    x_hbm, dy_hbm, wg_hbm, wu_hbm, wd_hbm, G, ss_out,
-    X, A, AT, H, DY, DYT, ACC, DT, ACT, WGU, WD, OWN, PART, OUT, SQ, SS,
+    x_hbm, dy_hbm, wg_hbm, wu_hbm, wd_hbm, md_hbm, G, ss_out, XA, ATS, PART, ACC,
+    H, DY, DT, ACT, WGU, WD, OWN, OUT, SQ, SS, sem_ahead,
     sem_in, sem_w, sem_d2d, sem_part, sem_up, sem_out, sem_g, sem_gsend, sem_share, sem_shared, sem_ss, sem_sssend,
 ):
+    X, A, AT, DYT = XA.at[0], XA.at[1], ATS.at[0], ATS.at[1]
     rep, dp = lax.axis_index("rep"), lax.axis_index("dp")
     z, core = lax.div(dp, 2), lax.rem(dp, 2)
 
@@ -355,9 +358,32 @@
 
     part_copy(jnp.int32(4 * STEPS - 2)).wait_send()
 
+    whole = pl.ds(0, AHEAD_UNITS * LANES)
+    ahead = (
+        pltpu.make_async_copy(wd_hbm.at[:, whole, :], XA, sem_ahead.at[0]),
+        pltpu.make_async_copy(wg_hbm.at[:, :, whole], ATS, sem_ahead.at[1]),
+        pltpu.make_async_copy(md_hbm.at[1, whole, :], ACC, sem_ahead.at[2]),
+    )
+    for copy in ahead:
+        copy.start()
+
+    def up_ahead(u, half):
+        columns = pl.ds(pl.multiple_of(lax.rem(u, PER_LAYER) * LANES, LANES), LANES)
+        rows = pl.ds(half * HALF, HALF)
+        return pltpu.make_async_copy(wu_hbm.at[jnp.where(u < PER_LAYER, 1, 0), rows, columns], PART.at[u, half], sem_ahead.at[3])
+
     @pl.loop(4 * STEPS, LAST)
     def _(n):
         communicate(n)
+
+        @pl.when(n >= SUMMED)
+        def _():
+            first = (n - SUMMED) * AT_A_TIME
+
+            @pl.loop(first, jnp.minimum(first + AT_A_TIME, UNITS))
+            def _(u):
+                for half in range(2):
+                    up_ahead(u, half).start()
 
         @pl.when((n == SUMMED) & (distance == 3))
         def _():
@@ -380,6 +406,11 @@
     pltpu.make_async_copy(everything, everything, sem_share.at[0]).wait()
     pltpu.make_async_copy(others, others, sem_shared.at[0]).wait()
 
+    for copy in ahead:
+        copy.wait()
+    landed = PART.at[:, pl.ds(0, 2)]
+    pltpu.make_async_copy(landed, landed, sem_ahead.at[3]).wait()
+
     for piece in range(2):
 
         @pl.when(jnp.logical_not((distance == 3) & (core == piece)))
@@ -394,7 +425,7 @@
     ss_out[...] = SS[0] + SS[1]
 
 
-def gradients(x, dy, w_gate, w_up, w_down):
+def gradients(x, dy, w_gate, w_up, w_down, m_down):
     hbm = pl.BlockSpec(memory_space=pl.ANY)
 
     def vmem(*shape):
@@ -403,21 +434,23 @@
     dma = pltpu.SemaphoreType.DMA
     return pl.pallas_call(
         gradient_kernel,
-        out_shape=(vmem(UNITS, 3, D, LANES), pltpu.VMEM((8, LANES), F32)),
-        in_specs=[hbm] * 5,
-        out_specs=(pl.BlockSpec(memory_space=pltpu.VMEM),) * 2,
+        out_shape=(
+            vmem(UNITS, 3, D, LANES), pltpu.VMEM((8, LANES), F32),
+            vmem(2, T, D), vmem(2, D, T), vmem(UNITS, 3, HALF, LANES), pltpu.VMEM((T, D), F32),
+        ),
+        in_specs=[hbm] * 6,
+        out_specs=(pl.BlockSpec(memory_space=pltpu.VMEM),) * 6,
         scratch_shapes=[
-            vmem(T, D), vmem(T, D), vmem(D, T), vmem(T, D), vmem(T, D), vmem(D, T),
-            pltpu.VMEM((T, D), F32),
+            vmem(T, D), vmem(T, D),
             vmem(T, 2 * TILE), vmem(T, TILE), vmem(2, D, 2 * TILE), vmem(2, TILE, D),
-            vmem(KEEP, 3, D, LANES), vmem(UNITS, 3, HALF, LANES), vmem(SLOTS, 3, HALF, LANES),
-            pltpu.VMEM((8, LANES), F32), pltpu.VMEM((2, 8, LANES), F32),
+            vmem(KEEP, 3, D, LANES), vmem(SLOTS, 3, HALF, LANES),
+            pltpu.VMEM((8, LANES), F32), pltpu.VMEM((2, 8, LANES), F32), dma((4,)),
             dma((T // 256 + 1,)), dma((2, 3)), dma((4,)), dma((UNITS,)), dma((UNITS,)), dma((SLOTS,)),
             dma((UNITS,)), dma((1,)), dma((1,)), dma((1,)), dma((2,)), dma((8,)),
         ],
-        compiler_params=pltpu.CompilerParams(collective_id=0, has_side_effects=True, vmem_limit_bytes=46 * 2**20),
+        compiler_params=pltpu.CompilerParams(collective_id=0, has_side_effects=True, vmem_limit_bytes=22 * 2**20),
         name="gradients",
-    )(x, dy, w_gate, w_up, w_down)
+    )(x, dy, w_gate, w_up, w_down, m_down)
 
 
 def update(w, m, v, g):
@@ -432,7 +465,7 @@
     return jnp.minimum(1.0, 0.5 * lax.rsqrt(total / (UNITS * 3 * D * LANES) + 1e-30))
 
 
-def adamw_kernel(ss, g, *refs):
+def adamw_kernel(ss, g, w_down_ahead, w_gate_ahead, w_up_ahead, m_down_ahead, *refs):
     w_in, m_in, v_in, w_new, m_new, v_new = (refs[i : i + 3] for i in range(0, 18, 3))
     WI, MI, VI, WO, DWI, DMI, DVI, DWO, sem_in, sem_out = refs[18:]
     factor = clip_factor(ss)
@@ -453,6 +486,19 @@
         pairs = ((w_in[k].at[at], w), (m_in[k].at[at], m), (v_in[k].at[at], v))
         return [pltpu.make_async_copy(src, dst, sem_in.at[slot, k, i]) for i, (src, dst) in enumerate(pairs)]
 
+    def is_ahead(u):
+        return lax.rem(u, PER_LAYER) < AHEAD_UNITS
+
+    def each_read(k, u, act):
+        w, m, v = reads(k, u)
+        act(v)
+        if k == 2:
+            pl.when(jnp.logical_not(is_ahead(u) & (u < PER_LAYER)))(lambda: act(m))
+        else:
+            act(m)
+        if k != 1:
+            pl.when(jnp.logical_not(is_ahead(u)))(lambda: act(w))
+
     def writes(k, u):
         slot, at, (_, m, v, w) = lax.rem(u, DEEP), place(k, u), buffers(k, u)
         pairs = ((w, w_new[k].at[at]), (m, m_new[k].at[at]), (v, v_new[k].at[at]))
@@ -460,8 +506,7 @@
 
     def start_reads(u):
         for k in range(3):
-            for copy in reads(k, u):
-                copy.start()
+            each_read(k, u, lambda copy: copy.start())
 
     for u in range(AHEAD):
         start_reads(jnp.int32(u))
@@ -480,9 +525,10 @@
 
             start_reads(later)
 
-        for k in range(3):
-            for copy in reads(k, u):
-                copy.wait()
+        layer = jnp.where(u < PER_LAYER, 1, 0)
+        columns = pl.ds(pl.multiple_of(lax.rem(u, PER_LAYER) * LANES, LANES), LANES)
+
+        def new_values(k, old_w, old_m):
             w, m, v, out = buffers(k, u)
             step = 160 if k < 2 else LANES
             for r in range(0, D, step):
@@ -490,7 +536,29 @@
                 gradient = g[u, k, piece, :]
                 at = (piece, slice(None)) if k < 2 else (slice(None), piece)
                 gradient = (gradient if k < 2 else gradient.T).astype(F32) * factor
-                out[at], m[at], v[at] = update(w[at].astype(F32), m[at], v[at], gradient)
+                out[at], m[at], v[at] = update(old_w(r, at).astype(F32), old_m(at), v[at], gradient)
+
+        def read_w(k):
+            return lambda r, at: buffers(k, u)[0][at]
+
+        def read_m(k):
+            return lambda at: buffers(k, u)[1][at]
+
+        def down_w(r, at):
+            return w_down_ahead[layer, columns, at[1]]
+
+        for k in range(3):
+            each_read(k, u, lambda copy: copy.wait())
+            if k == 0:
+                pl.when(is_ahead(u))(lambda: new_values(0, lambda r, at: w_gate_ahead[layer, at[0], columns], read_m(0)))
+                pl.when(jnp.logical_not(is_ahead(u)))(lambda: new_values(0, read_w(0), read_m(0)))
+            elif k == 1:
+                new_values(1, lambda r, at: w_up_ahead[u, r // HALF, r % HALF : r % HALF + 160, :], read_m(1))
+            else:
+                both = is_ahead(u) & (u < PER_LAYER)
+                pl.when(both)(lambda: new_values(2, down_w, lambda at: m_down_ahead[columns, at[1]]))
+                pl.when(is_ahead(u) & (u >= PER_LAYER))(lambda: new_values(2, down_w, read_m(2)))
+                pl.when(jnp.logical_not(is_ahead(u)))(lambda: new_values(2, read_w(2), read_m(2)))
             for copy in writes(k, u):
                 copy.start()
 
@@ -500,13 +568,13 @@
                 copy.wait()
 
 
-def adamw(ss, g, weights, m, v):
+def adamw(ss, g, ahead, weights, m, v):
     hbm = pl.BlockSpec(memory_space=pltpu.HBM)
-    ss, g = (pltpu.with_memory_space_constraint(a, pltpu.VMEM) for a in (ss, g))
+    near = [pltpu.with_memory_space_constraint(a, pltpu.VMEM) for a in (ss, g, *ahead)]
     dma = pltpu.SemaphoreType.DMA
     return pl.pallas_call(
         adamw_kernel,
-        in_specs=[pl.BlockSpec(memory_space=pltpu.VMEM)] * 2 + [hbm] * 9,
+        in_specs=[pl.BlockSpec(memory_space=pltpu.VMEM)] * 6 + [hbm] * 9,
         out_specs=(hbm,) * 9,
         out_shape=tuple(jax.ShapeDtypeStruct(a.shape, a.dtype) for a in (*weights, *m, *v)),
         scratch_shapes=[
@@ -515,16 +583,16 @@
             pltpu.VMEM((DEEP, LANES, D), BF16), pltpu.VMEM((DEEP, LANES, D), F32), pltpu.VMEM((DEEP, LANES, D), F32),
             pltpu.VMEM((DEEP, LANES, D), BF16), dma((DEEP, 3, 3)), dma((DEEP, 3, 3)),
         ],
-        compiler_params=pltpu.CompilerParams(vmem_limit_bytes=46 * 2**20),
+        compiler_params=pltpu.CompilerParams(vmem_limit_bytes=22 * 2**20),
         name="adamw",
-    )(ss, g, *weights, *m, *v)
+    )(*near, *weights, *m, *v)
 
 
 def solution(mesh):
     def step(x, dy, *arrays):
         weights, m, v = (arrays[i : i + 3] for i in (0, 3, 6))
-        g, ss = gradients(x, dy, *weights)
-        return adamw(ss, g, weights, m, v)
+        g, ss, *ahead = gradients(x, dy, *weights, m[2])
+        return adamw(ss, g, ahead, weights, m, v)
 
     return jax.shard_map(
         step,

time: 331 us -> 328 us (level)
  Pallas kernels: 331 us -> 327 us
    pallas_call x1, Pallas kernels: 60.9 us -> 54.9 us  [adamw(): pl.pallas_call(adamw_kernel, in_specs=[pl.BlockSpec(memory_space=pltpu.VM...]
where the time goes in v4:
time: 328 us
  Pallas kernels  327 us (100%)
    pallas_call x1, Pallas kernels, gradients(): pl.pallas_call(gradient_kernel, out_shape=(vmem(UNITS, 3, D, LANES), pltp...  272 us
    pallas_call x1, Pallas kernels, adamw(): pl.pallas_call(adamw_kernel, in_specs=[pl.BlockSpec(memory_space=pltpu.VM...  54.9 us

profile of v4, /device:TPU:0, one launch (start us, length us, event | category | flops | bytes accessed | tf_op | source)
XLA Modules:
  0.0 327.6 jit_solution(16190106840183255240)
XLA Ops:
  0.6 271.9 %gradients.1 = (bf16[38,3,640,128]{3,2,1,0:T(8,128)(2,1)S(1)}, f32[8,128]{1,0:T(8,128)S(1)}, bf16[2,2048,640]{2,1,0:T(8,128)(2,1)S(1)}, bf16[2,640,2048]{2,1,0:T...) custom-call(bf16[1,2048,640]{2,1,0:T(8,128)(2,1)} %x_hbm.1, ...), custom_call_target="tpu_custom_call" | custom-call | tf_op jit(solution)/shard_map/gradients/pallas_call | solution.py:435
  272.6 54.9 %adamw.1 = (bf16[2,640,2432]{2,1,0:T(8,128)(2,1)}, bf16[2,640,2432]{2,1,0:T(8,128)(2,1)}, bf16[2,2432,640]{2,1,0:T(8,128)(2,1)}, f32[2,640,2432]{2,1,0:T(8,128)}...) custom-call(f32[8,128]{1,0:T(8,128)S(1)} %get-tuple-element.15.ss, ...), custom_call_target="tpu_custom_call" | custom-call | tf_op jit(solution)/shard_map/adamw/pallas_call | solution.py:575

commit v5 on v4

--- a/solution.py
+++ b/solution.py
@@ -26,7 +26,7 @@
 LAST = SUMMED + 3 * BACK
 AT_A_TIME = -(-UNITS // (LAST - SUMMED))
 
-DEEP, AHEAD = 6, 3
+DEEP, AHEAD = 6, 4
 AHEAD_UNITS = T // LANES
 
 

time: 328 us -> 327 us (level)
  no operation moved by 1% of the time
where the time goes in v5:
time: 327 us
  Pallas kernels  326 us (100%)
    pallas_call x1, Pallas kernels, gradients(): pl.pallas_call(gradient_kernel, out_shape=(vmem(UNITS, 3, D, LANES), pltp...  272 us
    pallas_call x1, Pallas kernels, adamw(): pl.pallas_call(adamw_kernel, in_specs=[pl.BlockSpec(memory_space=pltpu.VM...  54.4 us

profile of v5, /device:TPU:0, one launch (start us, length us, event | category | flops | bytes accessed | tf_op | source)
XLA Modules:
  0.0 327.1 jit_solution(5184396073564733333)
XLA Ops:
  0.6 271.9 %gradients.1 = (bf16[38,3,640,128]{3,2,1,0:T(8,128)(2,1)S(1)}, f32[8,128]{1,0:T(8,128)S(1)}, bf16[2,2048,640]{2,1,0:T(8,128)(2,1)S(1)}, bf16[2,640,2048]{2,1,0:T...) custom-call(bf16[1,2048,640]{2,1,0:T(8,128)(2,1)} %x_hbm.1, ...), custom_call_target="tpu_custom_call" | custom-call | tf_op jit(solution)/shard_map/gradients/pallas_call | solution.py:435
  272.6 54.4 %adamw.1 = (bf16[2,640,2432]{2,1,0:T(8,128)(2,1)}, bf16[2,640,2432]{2,1,0:T(8,128)(2,1)}, bf16[2,2432,640]{2,1,0:T(8,128)(2,1)}, f32[2,640,2432]{2,1,0:T(8,128)}...) custom-call(f32[8,128]{1,0:T(8,128)S(1)} %get-tuple-element.15.ss, ...), custom_call_target="tpu_custom_call" | custom-call | tf_op jit(solution)/shard_map/adamw/pallas_call | solution.py:575

commit v6 on v5

--- a/solution.py
+++ b/solution.py
@@ -26,7 +26,7 @@
 LAST = SUMMED + 3 * BACK
 AT_A_TIME = -(-UNITS // (LAST - SUMMED))
 
-DEEP, AHEAD = 6, 4
+DEEP, AHEAD = 7, 4
 AHEAD_UNITS = T // LANES
 
 

time: 327 us -> 328 us (level)
  no operation moved by 1% of the time
where the time goes in v6:
time: 328 us
  Pallas kernels  327 us (100%)
    pallas_call x1, Pallas kernels, gradients(): pl.pallas_call(gradient_kernel, out_shape=(vmem(UNITS, 3, D, LANES), pltp...  272 us
    pallas_call x1, Pallas kernels, adamw(): pl.pallas_call(adamw_kernel, in_specs=[pl.BlockSpec(memory_space=pltpu.VM...  54.8 us

profile of v6, /device:TPU:0, one launch (start us, length us, event | category | flops | bytes accessed | tf_op | source)
XLA Modules:
  0.0 327.6 jit_solution(15076998872654940622)
XLA Ops:
  0.6 271.9 %gradients.1 = (bf16[38,3,640,128]{3,2,1,0:T(8,128)(2,1)S(1)}, f32[8,128]{1,0:T(8,128)S(1)}, bf16[2,2048,640]{2,1,0:T(8,128)(2,1)S(1)}, bf16[2,640,2048]{2,1,0:T...) custom-call(bf16[1,2048,640]{2,1,0:T(8,128)(2,1)} %x_hbm.1, ...), custom_call_target="tpu_custom_call" | custom-call | tf_op jit(solution)/shard_map/gradients/pallas_call | solution.py:435
  272.6 54.8 %adamw.1 = (bf16[2,640,2432]{2,1,0:T(8,128)(2,1)}, bf16[2,640,2432]{2,1,0:T(8,128)(2,1)}, bf16[2,2432,640]{2,1,0:T(8,128)(2,1)}, f32[2,640,2432]{2,1,0:T(8,128)}...) custom-call(f32[8,128]{1,0:T(8,128)S(1)} %get-tuple-element.15.ss, ...), custom_call_target="tpu_custom_call" | custom-call | tf_op jit(solution)/shard_map/adamw/pallas_call | solution.py:575
